TPU v7x, 256 devices: a whole 4x4x8 slice. The times are simulated.
256 devices in a mesh: grp: 16 (over z, x_lo), sp: 16 (over x_hi, y, core).
Axes of the slice: x: 4 (x_hi: 2, x_lo: 2; x = x_hi * 2 + x_lo), y: 4, z: 8, core: 2. Of those that a mesh axis runs over, the one named last changes fastest.
Arguments:
- query_rows: bfloat16 [32768, 4096], P(('grp', 'sp')), parts along dimension 0, may hold values from -250 to 250
- key_rows: bfloat16 [32768, 1024], P(('grp', 'sp')), parts along dimension 0, may hold values from -4 to 4
- value_rows: bfloat16 [32768, 1024], P(('grp', 'sp')), parts along dimension 0, may hold values from -6 to 6
- out_grad: bfloat16 [32768, 4096], P(('grp', 'sp')), parts along dimension 0, may hold values from -6 to 6
- question_lengths: int32 [128], P('grp'), parts along dimension 0, may hold values from 1 to 512, 1024 in all
Outputs:
- query_grad: bfloat16 [32768, 4096], P(('grp', 'sp')), parts along dimension 0
- key_grad: bfloat16 [32768, 1024], P(('grp', 'sp')), parts along dimension 0
- value_grad: bfloat16 [32768, 1024], P(('grp', 'sp')), parts along dimension 0
There are 16 independent parts, one for each index of `grp`. A program takes and returns all parts, laid end to end along the dimension named above; each array names one. Nothing has to cross between parts.
All inputs are finite; a program needn't handle non-finite values.
Results may differ from a plain program's by a relative error of at most 0.033.
Values may be sent and summed in bfloat16 or wider, within the bound.
A program may use at most 128 MiB of HBM per device.

v0:
```python
from functools import partial
from functools import reduce
import math

import jax
import jax.numpy as jnp
from jax import lax
from jax.sharding import PartitionSpec as P

HD = 128
QH = 32
KVH = 8


MASKED = -1e30


def widen(rows, copies):
    tokens = rows.shape[0]
    shaped = rows.reshape(tokens, KVH, 1, HD)
    return jnp.broadcast_to(shaped, (tokens, KVH, copies, HD)).reshape(tokens, KVH * copies * HD)


def segment_ids(question_lengths, length, doc_len):
    ends = jnp.cumsum(question_lengths)
    places = jnp.arange(length, dtype=jnp.int32)
    inside = jnp.sum((ends[None, :] <= (places - doc_len)[:, None]).astype(jnp.int32), axis=1)
    return jnp.where(places < doc_len, -1, inside)


def make_scores(query_block, key_block, visible, scaling):
    raw = (
        jnp.einsum("bkgd,skd->kgbs", query_block, key_block, preferred_element_type=jnp.float32)
        * scaling
    )
    return jnp.where(visible[None, None], raw, MASKED)


def weighted_values(probs_b, value_block):
    return jnp.einsum("kgbs,skd->bkgd", probs_b, value_block, preferred_element_type=jnp.float32)


def backward_block(probs, probs_b, delta, grad_block, query_block, key_block, value_block, scaling):
    value_part = jnp.einsum(
        "kgbs,bkgd->skd", probs_b, grad_block, preferred_element_type=jnp.float32
    )
    prob_grad = jnp.einsum(
        "bkgd,skd->kgbs", grad_block, value_block, preferred_element_type=jnp.float32
    )
    score_grad = (probs * (prob_grad - delta[..., None])).astype(jnp.bfloat16)
    query_part = jnp.einsum(
        "kgbs,skd->bkgd", score_grad, key_block, preferred_element_type=jnp.float32
    )
    key_part = (
        jnp.einsum("kgbs,bkgd->skd", score_grad, query_block, preferred_element_type=jnp.float32)
        * scaling
    )
    return (query_part, key_part, value_part)


def on_device(query_rows, key_rows, value_rows, out_grad, question_lengths):
    devices = lax.axis_size("sp")
    tokens = query_rows.shape[0]
    length = tokens * devices
    doc_len = length // 2
    block_len = min(512, length)
    block_count = length // block_len
    scaling = 1.0 / math.sqrt(HD)
    copies = max(KVH, devices) // KVH
    keys_local, values_local = (
        lax.all_to_all(widen(key_rows, copies), "sp", split_axis=1, concat_axis=0, tiled=True),
        lax.all_to_all(widen(value_rows, copies), "sp", split_axis=1, concat_axis=0, tiled=True),
    )
    queries_local, grads_local = (
        lax.all_to_all(query_rows, "sp", split_axis=1, concat_axis=0, tiled=True),
        lax.all_to_all(out_grad, "sp", split_axis=1, concat_axis=0, tiled=True),
    )
    key_heads = KVH * copies // devices
    per_group = QH // devices // key_heads
    queries = queries_local.reshape(length, key_heads, per_group, HD)
    grads = grads_local.reshape(length, key_heads, per_group, HD)
    keys = keys_local.reshape(length, key_heads, HD)
    values = values_local.reshape(length, key_heads, HD)
    segment = segment_ids(question_lengths, length, doc_len)
    places = jnp.arange(length, dtype=jnp.int32)
    query_shape = (block_len, key_heads, per_group, HD)
    key_shape = (block_len, key_heads, HD)
    key_sums = [jnp.zeros(key_shape, jnp.float32)] * block_count
    value_sums = [jnp.zeros(key_shape, jnp.float32)] * block_count
    query_parts = []
    for row_block in range(block_count):
        row_start = row_block * block_len
        query_block = queries[row_start : row_start + block_len]
        grad_block = grads[row_start : row_start + block_len]
        row_places = places[row_start : row_start + block_len]
        row_segment = segment[row_start : row_start + block_len]
        needs = []
        scores = []
        for col_block in range(row_block + 1):
            col_start = col_block * block_len
            col_places = places[col_start : col_start + block_len]
            col_segment = segment[col_start : col_start + block_len]
            visible = (col_places[None, :] <= row_places[:, None]) & (
                (col_places[None, :] < doc_len) | (col_segment[None, :] == row_segment[:, None])
            )
            needed = True
            needs.append(needed)
            scores.append(
                make_scores(query_block, keys[col_start : col_start + block_len], visible, scaling)
            )
        peak = reduce(jnp.maximum, [jnp.max(score, axis=3) for score in scores])
        total = reduce(
            jnp.add, [jnp.sum(jnp.exp(score - peak[..., None]), axis=3) for score in scores]
        )
        log_total = peak + jnp.log(total)
        probs = [jnp.exp(score - log_total[..., None]) for score in scores]
        probs_low = [single.astype(jnp.bfloat16) for single in probs]
        output = jnp.zeros(query_shape, jnp.float32)
        for col_block in range(row_block + 1):
            col_start = col_block * block_len
            output = output + weighted_values(
                probs_low[col_block], values[col_start : col_start + block_len]
            )
        output_low = output.astype(jnp.bfloat16)
        delta = jnp.einsum(
            "bkgd,bkgd->kgb", grad_block, output_low, preferred_element_type=jnp.float32
        )
        query_sum = jnp.zeros(query_shape, jnp.float32)
        for col_block in range(row_block + 1):
            col_start = col_block * block_len
            action = partial(
                backward_block,
                probs[col_block],
                probs_low[col_block],
                delta,
                grad_block,
                query_block,
                keys[col_start : col_start + block_len],
                values[col_start : col_start + block_len],
                scaling,
            )
            query_part, key_part, value_part = action()
            query_sum = query_sum + query_part
            key_sums[col_block] = key_sums[col_block] + key_part
            value_sums[col_block] = value_sums[col_block] + value_part
        query_parts.append((query_sum * scaling).astype(jnp.bfloat16))
    query_local = jnp.concatenate(query_parts, axis=0).reshape(length, key_heads * per_group * HD)
    key_local = jnp.concatenate(key_sums, axis=0).reshape(length, key_heads * HD)
    value_local = jnp.concatenate(value_sums, axis=0).reshape(length, key_heads * HD)
    query_grad = lax.all_to_all(query_local, "sp", split_axis=0, concat_axis=1, tiled=True)
    key_back, value_back = (
        lax.all_to_all(key_local, "sp", split_axis=0, concat_axis=1, tiled=True),
        lax.all_to_all(value_local, "sp", split_axis=0, concat_axis=1, tiled=True),
    )
    key_grad = (
        jnp.sum(key_back.reshape(tokens, KVH, copies, HD), axis=2)
        .reshape(tokens, KVH * HD)
        .astype(jnp.bfloat16)
    )
    value_grad = (
        jnp.sum(value_back.reshape(tokens, KVH, copies, HD), axis=2)
        .reshape(tokens, KVH * HD)
        .astype(jnp.bfloat16)
    )
    return (query_grad, key_grad, value_grad)


def solution(mesh):
    return jax.shard_map(
        on_device,
        mesh=mesh,
        in_specs=(
            P(("grp", "sp"), None),
            P(("grp", "sp"), None),
            P(("grp", "sp"), None),
            P(("grp", "sp"), None),
            P("grp"),
        ),
        out_specs=(P(("grp", "sp"), None), P(("grp", "sp"), None), P(("grp", "sp"), None)),
        check_vma=False,
    )
```

profile of v0, /device:TPU:1, one launch (start us, length us, event | category | flops | bytes accessed | tf_op | source)
XLA Modules:
  0.0 223.0 jit_solution(13801964207126556027)
XLA Ops:
  2.5 8.4 %all-to-all-start = ((bf16[128,16,128]{2,0,1:T(8,128)(2,1)}), bf16[128,16,128]{2,0,1:T(8,128)(2,1)S(1)}, u32[]{:S(2)}, u32[]{:S(2)}) async-start(bf16[128,16,128]{2,0,1:T(8,128)(2,1)} %bitcast.10), calls=%async_computation | async-start | bytes 1048576 | tf_op jit(solution)/shard_map/all_to_all | solution.py:71
  11.0 11.1 %all-to-all-done = bf16[128,16,128]{2,0,1:T(8,128)(2,1)S(1)} async-done(((bf16[128,16,128]{2,0,1:T(8,128)(2,1)}), bf16[128,16,128]{2,0,1:T(8,128)(2,1)S(1)}, u32[]{:S(2)}, u32[]{:S(2)}) %all-to-all-start) | async-done | bytes 524320 | tf_op jit(solution)/shard_map/all_to_all | solution.py:71
  23.0 4.6 %all-to-all-start.2 = ((bf16[128,16,128]{2,0,1:T(8,128)(2,1)}), bf16[128,16,128]{2,0,1:T(8,128)(2,1)S(1)}, u32[]{:S(2)}, u32[]{:S(2)}) async-start(bf16[128,16,128]{2,0,1:T(8,128)(2,1)} %bitcast.17), calls=%async_computation.2 | async-start | bytes 1048576 | tf_op jit(solution)/shard_map/all_to_all | solution.py:72
  27.7 1.1 copy.533
  28.8 2.3 %copy.532 = bf16[16,16,8,256]{3,2,0,1:T(8,128)(2,1)} copy(bf16[16,16,8,256]{3,2,1,0:T(8,128)(2,1)} %bitcast.578) | data formatting | bytes 2097152 | tf_op jit(solution)/shard_map/all_to_all | solution.py:76
  31.3 7.7 %all-to-all-done.2 = bf16[128,16,128]{2,0,1:T(8,128)(2,1)S(1)} async-done(((bf16[128,16,128]{2,0,1:T(8,128)(2,1)}), bf16[128,16,128]{2,0,1:T(8,128)(2,1)S(1)}, u32[]{:S(2)}, u32[]{:S(2)}) %all-to-all-start.2) | async-done | bytes 524320 | tf_op jit(solution)/shard_map/all_to_all | solution.py:72
  39.7 4.7 %all-to-all-start.1 = ((bf16[128,16,256]{2,0,1:T(8,128)(2,1)}), bf16[128,16,256]{2,0,1:T(8,128)(2,1)S(1)}, u32[]{:S(2)}, u32[]{:S(2)}) async-start(bf16[128,16,256]{2,0,1:T(8,128)(2,1)} %bitcast.532), calls=%async_computation.1 | async-start | bytes 2097152 | tf_op jit(solution)/shard_map/all_to_all | solution.py:75
  44.6 17.0 %all-to-all-done.1 = bf16[128,16,256]{2,0,1:T(8,128)(2,1)S(1)} async-done(((bf16[128,16,256]{2,0,1:T(8,128)(2,1)}), bf16[128,16,256]{2,0,1:T(8,128)(2,1)S(1)}, u32[]{:S(2)}, u32[]{:S(2)}) %all-to-all-start.1) | async-done | bytes 1048608 | tf_op jit(solution)/shard_map/all_to_all | solution.py:75
  61.6 4.4 %all-to-all-start.3 = ((bf16[128,16,256]{2,0,1:T(8,128)(2,1)}), bf16[128,16,256]{2,0,1:T(8,128)(2,1)S(1)}, u32[]{:S(2)}, u32[]{:S(2)}) async-start(bf16[128,16,256]{2,0,1:T(8,128)(2,1)} %bitcast.531), calls=%async_computation.3 | async-start | bytes 2097152 | tf_op jit(solution)/shard_map/all_to_all | solution.py:76
  66.0 4.4 %or_and_fusion.9 = (pred[512,512]{0,1:T(8,128)(4,1)}, pred[512,512]{0,1:T(8,128)(4,1)}, pred[512,512]{0,1:T(8,128)(4,1)}, pred[512,512]{0,1:T(8,128)(4,1)}, pred...) fusion(s32[512]{0:T(512)S(1)} %get-tuple-element.43, ...), kind=kLoop, calls=%fused_computation.181 | loop fusion | flops 10485760 | bytes 2639872 | tf_op jit(solution)/shard_map/and | solution.py:103
  72.9 10.4 %all-to-all-done.3 = bf16[128,16,256]{2,0,1:T(8,128)(2,1)S(1)} async-done(((bf16[128,16,256]{2,0,1:T(8,128)(2,1)}), bf16[128,16,256]{2,0,1:T(8,128)(2,1)S(1)}, u32[]{:S(2)}, u32[]{:S(2)}) %all-to-all-start.3) | async-done | bytes 1048608 | tf_op jit(solution)/shard_map/all_to_all | solution.py:76
  84.8 1.8 fusion.164
  88.1 1.1 convolution_bitcast_fusion.4
  89.2 1.1 convolution_bitcast_fusion.7
  92.7 3.2 %fusion.34 = bf16[2,512,512]{1,2,0:T(8,128)(2,1)} fusion(bf16[512,128,1]{1,0,2:T(8,128)(2,1)S(1)} %bitcast.542, f32[1,2,512,512]{2,3,1,0:T(8,128)} %copy-done.7, f32[2,512]{1,0:T(2,128)S(1)} %copy.400, f32[2,512]{1,0:T(2,128)S(1)} %log_add_fusion.1, bf16[512,2,128]{2,1,0:T(2,128)(2,1)S(1)} %reshape.1432), kind=kOutput, calls=%fused_computation.74 | convolution fusion | flops 136314880 | bytes 3547136 | tf_op jit(solution)/shard_map/bkgd,skd->kgbs/dot_general | solution.py:47
  96.0 1.5 fusion.33
  97.5 1.5 fusion.35
  99.0 1.1 reshape.1423
  100.2 1.5 fusion.167
  103.5 1.2 convolution_bitcast_fusion.8
  106.0 3.3 %fusion.31 = bf16[2,512,512]{1,2,0:T(8,128)(2,1)} fusion(bf16[512,128,1]{1,0,2:T(8,128)(2,1)S(1)} %bitcast.536, f32[1,2,512,512]{2,3,1,0:T(8,128)} %copy-done.8, f32[2,512]{1,0:T(2,128)S(1)} %copy.388, f32[2,512]{1,0:T(2,128)S(1)} %log_add_fusion.2, bf16[512,2,128]{2,1,0:T(2,128)(2,1)S(1)} %reshape.1423), kind=kOutput, calls=%fused_computation.71 | convolution fusion | flops 136314880 | bytes 3547136 | tf_op jit(solution)/shard_map/bkgd,skd->kgbs/dot_general | solution.py:47
  109.3 1.9 fusion.32
  111.2 1.1 reshape.1443
  112.4 1.6 fusion.162
  116.6 1.2 exponential_reduce_fusion.2
  117.8 1.2 convolution_bitcast_fusion
  119.0 1.1 convolution_bitcast_fusion.1
  120.1 1.2 convolution_bitcast_fusion.3
  121.3 1.2 convolution_bitcast_fusion.6
  124.9 1.4 multiply_reduce_fusion
  126.3 1.1 copy.414
  127.4 3.2 %fusion.37 = bf16[2,512,512]{1,2,0:T(8,128)(2,1)} fusion(bf16[512,128,1]{1,0,2:T(8,128)(2,1)S(1)} %bitcast.546, f32[1,2,512,512]{2,3,1,0:T(8,128)} %copy-done.15, f32[2,512]{1,0:T(2,128)S(1)} %copy.414, f32[2,512]{1,0:T(2,128)S(1)} %log_add_fusion, bf16[512,2,128]{2,1,0:T(2,128)(2,1)S(1)} %reshape.1443), kind=kOutput, calls=%fused_computation.77 | convolution fusion | flops 136314880 | bytes 3547136 | tf_op jit(solution)/shard_map/bkgd,skd->kgbs/dot_general | solution.py:47
  130.6 1.5 fusion.38
  132.5 1.5 fusion.39
  134.4 1.5 fusion.36
  135.8 1.0 reshape.1415
  136.9 1.1 reshape.1417
  138.0 1.5 fusion.169
  141.8 2.2 fusion.30
  144.1 1.2 fusion.59
  145.3 1.3 fusion.171
  146.6 1.3 fusion.170
  148.9 1.1 copy-done.17
  151.1 1.1 pad_maximum_fusion.2
  152.2 5.2 %all-to-all-start.6 = ((f32[16,128,128]{2,1,0:T(8,128)}), f32[16,128,128]{2,1,0:T(8,128)}, u32[]{:S(2)}, u32[]{:S(2)}) async-start(f32[16,128,128]{2,1,0:T(8,128)} %bitcast.194), calls=%async_computation.6 | async-start | bytes 2097152 | tf_op jit(solution)/shard_map/all_to_all | solution.py:153
  157.9 1.6 convolution_add_fusion.7
  162.6 1.1 pad_maximum_fusion
  163.7 1.1 convolution_bitcast_fusion.17
  164.8 2.2 %copy.344 = bf16[2048,1,2,128]{0,3,2,1:T(8,128)(2,1)} copy(bf16[2048,1,2,128]{3,0,2,1:T(8,128)(2,1)} %pad_maximum_fusion) | data formatting | bytes 2097152 | tf_op jit(solution)/shard_map/concatenate | solution.py:147
  167.1 1.5 copy.423
  168.6 1.3 copy.345
  169.9 1.1 convolution_bitcast_fusion.14
  171.0 1.1 convolution_bitcast_fusion.18
  172.1 1.1 convolution_bitcast_fusion.16
  173.3 1.1 convolution_bitcast_fusion.13
  174.4 1.1 fusion.58
  175.6 7.3 %all-to-all-start.4 = ((bf16[16,128,256]{1,2,0:T(8,128)(2,1)}), bf16[16,128,256]{1,2,0:T(8,128)(2,1)}, u32[]{:S(2)}, u32[]{:S(2)}) async-start(bf16[16,128,256]{1,2,0:T(8,128)(2,1)} %copy.345), calls=%async_computation.4 | async-start | bytes 2097152 | tf_op jit(solution)/shard_map/all_to_all | solution.py:150
  183.4 1.5 fusion.71
  186.0 1.0 pad_maximum_fusion.1
  187.0 13.1 %all-to-all-done.4 = bf16[16,128,256]{1,2,0:T(8,128)(2,1)} async-done(((bf16[16,128,256]{1,2,0:T(8,128)(2,1)}), bf16[16,128,256]{1,2,0:T(8,128)(2,1)}, u32[]{:S(2)}, u32[]{:S(2)}) %all-to-all-start.4) | async-done | bytes 1048608 | tf_op jit(solution)/shard_map/all_to_all | solution.py:150
  200.1 4.5 %all-to-all-start.5 = ((f32[16,128,128]{2,1,0:T(8,128)}), f32[16,128,128]{2,1,0:T(8,128)S(1)}, u32[]{:S(2)}, u32[]{:S(2)}) async-start(f32[16,128,128]{2,1,0:T(8,128)} %bitcast.168), calls=%async_computation.5 | async-start | bytes 2097152 | tf_op jit(solution)/shard_map/all_to_all | solution.py:152
  204.5 1.3 bitcast_reduce_fusion
  206.9 2.3 %copy.368 = bf16[128,4096]{1,0:T(8,128)(2,1)} copy(bf16[128,4096]{0,1:T(8,128)(2,1)} %bitcast.145) | data formatting | bytes 2097152
  209.2 12.5 %all-to-all-done.5 = f32[16,128,128]{2,1,0:T(8,128)S(1)} async-done(((f32[16,128,128]{2,1,0:T(8,128)}), f32[16,128,128]{2,1,0:T(8,128)S(1)}, u32[]{:S(2)}, u32[]{:S(2)}) %all-to-all-start.5) | async-done | bytes 1048608 | tf_op jit(solution)/shard_map/all_to_all | solution.py:152
  (238 shorter events, 31.9 us)
Async XLA Ops:
  0.6 10.3 %copy-start.82 = (bf16[128,1024]{1,0:T(8,128)(2,1)S(1)}, bf16[128,1024]{1,0:T(8,128)(2,1)}, u32[]{:S(2)}) copy-start(bf16[128,1024]{1,0:T(8,128)(2,1)} %param.7) | copy-start | bytes 786436
  1.6 26.0 %copy-start.59 = (bf16[128,4096]{1,0:T(8,128)(2,1)S(1)}, bf16[128,4096]{1,0:T(8,128)(2,1)}, u32[]{:S(2)}) copy-start(bf16[128,4096]{1,0:T(8,128)(2,1)} %param.5) | copy-start | bytes 3145732
  2.5 19.6 %all-to-all-start = ((bf16[128,16,128]{2,0,1:T(8,128)(2,1)}), bf16[128,16,128]{2,0,1:T(8,128)(2,1)S(1)}, u32[]{:S(2)}, u32[]{:S(2)}) async-start(bf16[128,16,128]{2,0,1:T(8,128)(2,1)} %bitcast.10), calls=%async_computation | async-start | bytes 1048576 | tf_op jit(solution)/shard_map/all_to_all | solution.py:71
  23.0 15.9 %all-to-all-start.2 = ((bf16[128,16,128]{2,0,1:T(8,128)(2,1)}), bf16[128,16,128]{2,0,1:T(8,128)(2,1)S(1)}, u32[]{:S(2)}, u32[]{:S(2)}) async-start(bf16[128,16,128]{2,0,1:T(8,128)(2,1)} %bitcast.17), calls=%async_computation.2 | async-start | bytes 1048576 | tf_op jit(solution)/shard_map/all_to_all | solution.py:72
  27.7 3.4 %copy-start.83 = (s32[8]{0:T(128)S(1)}, s32[8]{0:T(128)}, u32[]{:S(2)}) copy-start(s32[8]{0:T(128)} %param.9) | copy-start | bytes 100
  39.7 21.9 %all-to-all-start.1 = ((bf16[128,16,256]{2,0,1:T(8,128)(2,1)}), bf16[128,16,256]{2,0,1:T(8,128)(2,1)S(1)}, u32[]{:S(2)}, u32[]{:S(2)}) async-start(bf16[128,16,256]{2,0,1:T(8,128)(2,1)} %bitcast.532), calls=%async_computation.1 | async-start | bytes 2097152 | tf_op jit(solution)/shard_map/all_to_all | solution.py:75
  61.6 21.6 %all-to-all-start.3 = ((bf16[128,16,256]{2,0,1:T(8,128)(2,1)}), bf16[128,16,256]{2,0,1:T(8,128)(2,1)S(1)}, u32[]{:S(2)}, u32[]{:S(2)}) async-start(bf16[128,16,256]{2,0,1:T(8,128)(2,1)} %bitcast.531), calls=%async_computation.3 | async-start | bytes 2097152 | tf_op jit(solution)/shard_map/all_to_all | solution.py:76
  66.0 5.1 %copy-start.46 = (bf16[128,16,128]{2,0,1:T(8,128)(2,1)S(1)}, bf16[128,16,128]{2,0,1:T(8,128)(2,1)}, u32[]{:S(2)}) copy-start(bf16[128,16,128]{2,0,1:T(8,128)(2,1)} %copy-done.45) | copy-start | bytes 1572868
  71.1 13.7 %copy-start.52 = (bf16[4,128,128]{2,1,0:T(8,128)(2,1)}, bf16[4,128,128]{2,1,0:T(8,128)(2,1)S(1)}, u32[]{:S(2)}) copy-start(bf16[4,128,128]{2,1,0:T(8,128)(2,1)S(1)} %get-tuple-element.38) | copy-start | bytes 393220
  71.1 29.0 %copy-start.40 = (bf16[4,128,128]{2,1,0:T(8,128)(2,1)}, bf16[4,128,128]{2,1,0:T(8,128)(2,1)S(1)}, u32[]{:S(2)}) copy-start(bf16[4,128,128]{2,1,0:T(8,128)(2,1)S(1)} %get-tuple-element.39) | copy-start | bytes 393220
  71.1 30.6 %copy-start.48 = (bf16[4,128,128]{2,1,0:T(8,128)(2,1)}, bf16[4,128,128]{2,1,0:T(8,128)(2,1)S(1)}, u32[]{:S(2)}) copy-start(bf16[4,128,128]{2,1,0:T(8,128)(2,1)S(1)} %get-tuple-element.36) | copy-start | bytes 393220
  72.8 11.4 %copy-start.81 = (pred[512,512]{0,1:T(8,128)(4,1)S(1)}, pred[512,512]{0,1:T(8,128)(4,1)}, u32[]{:S(2)}) copy-start(pred[512,512]{0,1:T(8,128)(4,1)} %get-tuple-element.45) | copy-start | bytes 786436
  72.8 13.8 %copy-start.37 = (bf16[512,2,128]{2,1,0:T(2,128)(2,1)}, bf16[512,2,128]{2,1,0:T(2,128)(2,1)S(1)}, u32[]{:S(2)}) copy-start(bf16[512,2,128]{2,1,0:T(2,128)(2,1)S(1)} %reshape.1430) | copy-start | bytes 786436
  84.8 5.6 %copy-start.5 = (f32[1,2,512,512]{2,3,1,0:T(8,128)}, f32[1,2,512,512]{2,3,1,0:T(8,128)S(1)}, u32[]{:S(2)}) copy-start(f32[1,2,512,512]{2,3,1,0:T(8,128)S(1)} %get-tuple-element.65) | copy-start | bytes 6291460
  84.8 1.8 copy-start.80
  87.2 3.7 %copy-start.7 = (f32[1,2,512,512]{2,3,1,0:T(8,128)}, f32[1,2,512,512]{2,3,1,0:T(8,128)S(1)}, u32[]{:S(2)}) copy-start(f32[1,2,512,512]{2,3,1,0:T(8,128)S(1)} %get-tuple-element.67) | copy-start | bytes 6291460
  92.7 3.2 %copy-start.6 = (f32[1,2,512,512]{2,3,1,0:T(8,128)S(1)}, f32[1,2,512,512]{2,3,1,0:T(8,128)}, u32[]{:S(2)}) copy-start(f32[1,2,512,512]{2,3,1,0:T(8,128)} %copy-done.5) | copy-start | bytes 6291460
  99.0 3.3 %copy-start.42 = (bf16[512,2,128]{2,1,0:T(2,128)(2,1)}, bf16[512,2,128]{2,1,0:T(2,128)(2,1)S(1)}, u32[]{:S(2)}) copy-start(bf16[512,2,128]{2,1,0:T(2,128)(2,1)S(1)} %reshape.1421) | copy-start | bytes 786436
  102.3 2.3 %copy-start.2 = (f32[1,2,512,512]{2,3,1,0:T(8,128)}, f32[1,2,512,512]{2,3,1,0:T(8,128)S(1)}, u32[]{:S(2)}) copy-start(f32[1,2,512,512]{2,3,1,0:T(8,128)S(1)} %get-tuple-element.71) | copy-start | bytes 6291460
  106.0 3.3 %copy-start.3 = (f32[1,2,512,512]{2,3,1,0:T(8,128)S(1)}, f32[1,2,512,512]{2,3,1,0:T(8,128)}, u32[]{:S(2)}) copy-start(f32[1,2,512,512]{2,3,1,0:T(8,128)} %copy-done.2) | copy-start | bytes 6291460
  109.3 1.9 copy-start.68
  111.2 4.7 %copy-start.35 = (bf16[512,2,128]{2,1,0:T(2,128)(2,1)}, bf16[512,2,128]{2,1,0:T(2,128)(2,1)S(1)}, u32[]{:S(2)}) copy-start(bf16[512,2,128]{2,1,0:T(2,128)(2,1)S(1)} %reshape.1441) | copy-start | bytes 786436
  114.0 8.5 %copy-start.9 = (f32[1,2,512,512]{2,3,1,0:T(8,128)}, f32[1,2,512,512]{2,3,1,0:T(8,128)S(1)}, u32[]{:S(2)}) copy-start(f32[1,2,512,512]{2,3,1,0:T(8,128)S(1)} %get-tuple-element.59) | copy-start | bytes 6291460
  114.6 8.9 %copy-start.11 = (f32[1,2,512,512]{2,3,1,0:T(8,128)}, f32[1,2,512,512]{2,3,1,0:T(8,128)S(1)}, u32[]{:S(2)}) copy-start(f32[1,2,512,512]{2,3,1,0:T(8,128)S(1)} %get-tuple-element.57) | copy-start | bytes 6291460
  115.9 7.1 %copy-start.15 = (f32[1,2,512,512]{2,3,1,0:T(8,128)}, f32[1,2,512,512]{2,3,1,0:T(8,128)S(1)}, u32[]{:S(2)}) copy-start(f32[1,2,512,512]{2,3,1,0:T(8,128)S(1)} %get-tuple-element.61) | copy-start | bytes 6291460
  116.6 7.5 %copy-start.13 = (f32[1,2,512,512]{2,3,1,0:T(8,128)}, f32[1,2,512,512]{2,3,1,0:T(8,128)S(1)}, u32[]{:S(2)}) copy-start(f32[1,2,512,512]{2,3,1,0:T(8,128)S(1)} %get-tuple-element.55) | copy-start | bytes 6291460
  127.4 3.2 %copy-start.12 = (f32[1,2,512,512]{2,3,1,0:T(8,128)S(1)}, f32[1,2,512,512]{2,3,1,0:T(8,128)}, u32[]{:S(2)}) copy-start(f32[1,2,512,512]{2,3,1,0:T(8,128)} %copy-done.11) | copy-start | bytes 6291460
  130.6 1.9 copy-start.14
  132.5 1.9 copy-start.10
  134.4 3.6 %copy-start.41 = (bf16[4,128,128]{2,1,0:T(8,128)(2,1)S(1)}, bf16[4,128,128]{2,1,0:T(8,128)(2,1)}, u32[]{:S(2)}) copy-start(bf16[4,128,128]{2,1,0:T(8,128)(2,1)} %copy-done.40) | copy-start | bytes 393220
  136.9 3.0 %copy-start.57 = (bf16[512,2,128]{2,1,0:T(2,128)(2,1)}, bf16[512,2,128]{2,1,0:T(2,128)(2,1)S(1)}, u32[]{:S(2)}) copy-start(bf16[512,2,128]{2,1,0:T(2,128)(2,1)S(1)} %reshape.1415) | copy-start | bytes 786436
  141.8 3.4 %copy-start.20 = (bf16[2,512,512]{1,2,0:T(8,128)(2,1)S(1)}, bf16[2,512,512]{1,2,0:T(8,128)(2,1)}, u32[]{:S(2)}) copy-start(bf16[2,512,512]{1,2,0:T(8,128)(2,1)} %fusion.33) | copy-start | bytes 3145732
  144.0 3.8 %copy-start.31 = (bf16[2,512,512]{1,2,0:T(8,128)(2,1)}, bf16[2,512,512]{1,2,0:T(8,128)(2,1)S(1)}, u32[]{:S(2)}) copy-start(bf16[2,512,512]{1,2,0:T(8,128)(2,1)S(1)} %fusion.30) | copy-start | bytes 3145732
  144.1 2.5 %copy-start.23 = (bf16[2,512,512]{1,2,0:T(8,128)(2,1)S(1)}, bf16[2,512,512]{1,2,0:T(8,128)(2,1)}, u32[]{:S(2)}) copy-start(bf16[2,512,512]{1,2,0:T(8,128)(2,1)} %fusion.31) | copy-start | bytes 3145732
  144.1 3.8 %copy-start.67 = (f32[512,128]{1,0:T(8,128)S(1)}, f32[512,128]{1,0:T(8,128)}, u32[]{:S(2)}) copy-start(f32[512,128]{1,0:T(8,128)} %convolution_bitcast_fusion.1) | copy-start | bytes 786436
  146.6 1.8 copy-start.55
  146.6 1.8 copy-start.56
  151.1 6.3 %copy-start.33 = (bf16[2,512,512]{1,2,0:T(8,128)(2,1)S(1)}, bf16[2,512,512]{1,2,0:T(8,128)(2,1)}, u32[]{:S(2)}) copy-start(bf16[2,512,512]{1,2,0:T(8,128)(2,1)} %fusion.36) | copy-start | bytes 3145732
  152.2 5.7 %copy-start.19 = (bf16[2,512,512]{1,2,0:T(8,128)(2,1)S(1)}, bf16[2,512,512]{1,2,0:T(8,128)(2,1)}, u32[]{:S(2)}) copy-start(bf16[2,512,512]{1,2,0:T(8,128)(2,1)} %fusion.34) | copy-start | bytes 3145732
  152.2 5.7 %copy-start.50 = (bf16[4,128,128]{2,1,0:T(8,128)(2,1)S(1)}, bf16[4,128,128]{2,1,0:T(8,128)(2,1)}, u32[]{:S(2)}) copy-start(bf16[4,128,128]{2,1,0:T(8,128)(2,1)} %copy-done.48) | copy-start | bytes 393220
  152.2 23.4 %all-to-all-start.6 = ((f32[16,128,128]{2,1,0:T(8,128)}), f32[16,128,128]{2,1,0:T(8,128)}, u32[]{:S(2)}, u32[]{:S(2)}) async-start(f32[16,128,128]{2,1,0:T(8,128)} %bitcast.194), calls=%async_computation.6 | async-start | bytes 2097152 | tf_op jit(solution)/shard_map/all_to_all | solution.py:153
  157.4 2.2 copy-start.18
  157.4 2.2 copy-start.54
  157.9 2.2 copy-start.22
  157.9 2.2 copy-start.47
  167.1 2.8 %copy-start.39 = (bf16[512,2,128]{2,1,0:T(2,128)(2,1)S(1)}, bf16[512,2,128]{2,1,0:T(2,128)(2,1)}, u32[]{:S(2)}) copy-start(bf16[512,2,128]{2,1,0:T(2,128)(2,1)} %copy-done.37) | copy-start | bytes 786436
  168.6 2.4 %copy-start.24 = (bf16[2,512,512]{1,2,0:T(8,128)(2,1)S(1)}, bf16[2,512,512]{1,2,0:T(8,128)(2,1)}, u32[]{:S(2)}) copy-start(bf16[2,512,512]{1,2,0:T(8,128)(2,1)} %fusion.31) | copy-start | bytes 3145732
  168.6 2.4 %copy-start.43 = (bf16[512,2,128]{2,1,0:T(2,128)(2,1)S(1)}, bf16[512,2,128]{2,1,0:T(2,128)(2,1)}, u32[]{:S(2)}) copy-start(bf16[512,2,128]{2,1,0:T(2,128)(2,1)} %copy-done.42) | copy-start | bytes 786436
  169.9 2.3 %copy-start.34 = (bf16[2,512,512]{1,2,0:T(8,128)(2,1)S(1)}, bf16[2,512,512]{1,2,0:T(8,128)(2,1)}, u32[]{:S(2)}) copy-start(bf16[2,512,512]{1,2,0:T(8,128)(2,1)} %fusion.36) | copy-start | bytes 3145732
  169.9 2.3 %copy-start.36 = (bf16[512,2,128]{2,1,0:T(2,128)(2,1)S(1)}, bf16[512,2,128]{2,1,0:T(2,128)(2,1)}, u32[]{:S(2)}) copy-start(bf16[512,2,128]{2,1,0:T(2,128)(2,1)} %copy-done.35) | copy-start | bytes 786436
  169.9 3.4 %copy-start.28 = (bf16[2,512,512]{1,2,0:T(8,128)(2,1)S(1)}, bf16[2,512,512]{1,2,0:T(8,128)(2,1)}, u32[]{:S(2)}) copy-start(bf16[2,512,512]{1,2,0:T(8,128)(2,1)} %fusion.37) | copy-start | bytes 3145732
  171.0 3.4 %copy-start.30 = (bf16[2,512,512]{1,2,0:T(8,128)(2,1)S(1)}, bf16[2,512,512]{1,2,0:T(8,128)(2,1)}, u32[]{:S(2)}) copy-start(bf16[2,512,512]{1,2,0:T(8,128)(2,1)} %fusion.39) | copy-start | bytes 3145732
  174.4 8.5 %copy-start.26 = (bf16[2,512,512]{1,2,0:T(8,128)(2,1)S(1)}, bf16[2,512,512]{1,2,0:T(8,128)(2,1)}, u32[]{:S(2)}) copy-start(bf16[2,512,512]{1,2,0:T(8,128)(2,1)} %fusion.38) | copy-start | bytes 3145732
  175.6 24.5 %all-to-all-start.4 = ((bf16[16,128,256]{1,2,0:T(8,128)(2,1)}), bf16[16,128,256]{1,2,0:T(8,128)(2,1)}, u32[]{:S(2)}, u32[]{:S(2)}) async-start(bf16[16,128,256]{1,2,0:T(8,128)(2,1)} %copy.345), calls=%async_computation.4 | async-start | bytes 2097152 | tf_op jit(solution)/shard_map/all_to_all | solution.py:150
  182.9 2.1 copy-start.44
  182.9 2.1 copy-start.72
  182.9 2.1 copy-start.73
  183.4 2.1 copy-start.32
  183.4 2.1 copy-start.58
  183.4 2.1 copy-start.60
  183.4 2.1 copy-start.61
  183.4 2.1 copy-start.62
  200.1 21.6 %all-to-all-start.5 = ((f32[16,128,128]{2,1,0:T(8,128)}), f32[16,128,128]{2,1,0:T(8,128)S(1)}, u32[]{:S(2)}, u32[]{:S(2)}) async-start(f32[16,128,128]{2,1,0:T(8,128)} %bitcast.168), calls=%async_computation.5 | async-start | bytes 2097152 | tf_op jit(solution)/shard_map/all_to_all | solution.py:152
  206.9 15.9 %copy-start.1 = (bf16[128,1024]{1,0:T(8,128)(2,1)S(1)}, bf16[128,1024]{1,0:T(8,128)(2,1)}, u32[]{:S(2)}) copy-start(bf16[128,1024]{1,0:T(8,128)(2,1)} %param.6) | copy-start | bytes 786436
  (27 other events, 37.0 us)
where the time goes:
time: 227 us; the launch traced here: 223 us
  waiting for transfers between devices  71.7 us (32%)
  matrix products  63.5 us (28%)
  starting transfers between devices  39.2 us (17%)
  local copies, waits for them, and re-layouts  30.7 us (14%)
  other arithmetic  15.9 us (7%)
    dot_general x10, matrix products, backward_block(): jnp.einsum('bkgd,skd->kgbs', grad_block, value_block, preferred_element_t...  21.3 us
    all_to_all x1, waiting for transfers between devices, on_device(): lax.all_to_all(query_rows, 'sp', split_axis=1, concat_axis=0, tiled=True)  17 us
    all_to_all x1, waiting for transfers between devices, on_device(): lax.all_to_all(query_local, 'sp', split_axis=0, concat_axis=1, tiled=True)  13.1 us
    all_to_all x1, waiting for transfers between devices, on_device(): lax.all_to_all(key_local, 'sp', split_axis=0, concat_axis=1, tiled=True)  12.5 us
    unnamed x172, local copies, waits for them, and re-layouts  12.3 us
    all_to_all x1, waiting for transfers between devices, on_device(): lax.all_to_all(widen(key_rows, copies), 'sp', split_axis=1, concat_axis=0...  11.1 us
    all_to_all x1, waiting for transfers between devices, on_device(): lax.all_to_all(out_grad, 'sp', split_axis=1, concat_axis=0, tiled=True)  10.4 us
    dot_general x10, matrix products, make_scores(): jnp.einsum('bkgd,skd->kgbs', query_block, key_block, preferred_element_ty...  9.8 us
  transfers between devices with their start and end apart: 7, of which 6 were waited for; matrix products, arithmetic and copies ran while one was open for 16% of the time, Pallas kernels for 0%

commit v1 on v0

v1 whole, which is shorter than its diff:
```python
import functools
import math

import jax
import jax.numpy as jnp
from jax import lax
from jax.experimental import pallas as pl
from jax.experimental.pallas import tpu as pltpu
from jax.sharding import PartitionSpec as P

HD = 128
QH = 32
KVH = 8
SEQ = 2048
DOC = 1024
NQ = 8
TOK = 128
BLK = 256
DEVS = 16
MASKED = -1e30
MESH = pl.DeviceIdType.MESH
BF = jnp.bfloat16
F32 = jnp.float32

PARTNERS = tuple(
    (a, b, c)
    for c in (0, 1)
    for a, b in ((1, 2), (1, 1), (0, 2), (1, 3), (1, 0), (0, 1), (0, 3), (0, 0))
    if (a, b, c) != (0, 0, 0)
)


def dot_t(a, b):
    return lax.dot_general(a, b, (((1,), (1,)), ((), ())), preferred_element_type=F32)


def dot_n(a, b):
    return lax.dot_general(a, b, (((1,), (0,)), ((), ())), preferred_element_type=F32)


def fold(x, op):
    return op(x.reshape(x.shape[0] // 8, 8, x.shape[1]), axis=0)


def kernel(
    lens,
    q_hbm,
    k_hbm,
    v_hbm,
    do_hbm,
    dq_out,
    dk_out,
    dv_out,
    qb,
    dob,
    kb,
    vb,
    kt,
    s_buf,
    dp_buf,
    dka,
    dva,
    dqb,
    part,
    fin,
    send_kv,
    recv_kv,
    send_q,
    recv_q,
    relay_kv,
    send_dq,
    recv_dq,
    send_part,
    recv_part,
    send_fin,
    recv_fin,
):
    grp = lax.axis_index("grp")
    me = lax.axis_index("sp")
    far = me // 8
    yy = (me // 2) % 4
    core = me % 2
    chip = me // 2
    other = chip * 2 + 1 - core
    scaling = 1.0 / math.sqrt(HD)
    to_log2 = scaling * math.log2(math.e)

    def partner(step):
        a, b, c = step
        return ((far + a) % 2) * 8 + ((yy + b) % 4) * 2 + (core + c) % 2

    def lanes(index, width=HD):
        return pl.ds(pl.multiple_of(index * width, width), width)

    def rows(index, width=TOK):
        return pl.ds(pl.multiple_of(index * width, width), width)

    def remote(src, dst, ss, rs, dev):
        return pltpu.make_async_remote_copy(
            src_ref=src, dst_ref=dst, send_sem=ss, recv_sem=rs, device_id=(grp, dev), device_id_type=MESH
        )

    barrier = pltpu.get_barrier_semaphore()
    for step in PARTNERS:
        pl.semaphore_signal(barrier, inc=1, device_id=(grp, partner(step)), device_id_type=MESH)
    pl.semaphore_wait(barrier, len(PARTNERS))

    kv = ((k_hbm, kb), (v_hbm, vb))
    qd = ((q_hbm, qb), (do_hbm, dob))

    for step in PARTNERS:
        if step[2] == 0:
            dev = partner(step)
            for t, (src, dst) in enumerate(kv):
                remote(
                    src.at[:, lanes(dev // 2)], dst.at[rows(me)], send_kv.at[t, dev], recv_kv.at[t, me], dev
                ).start()
    for t, (src, dst) in enumerate(kv):
        pltpu.make_async_copy(src.at[:, lanes(chip)], dst.at[rows(me)], recv_kv.at[t, me]).start()
        remote(
            src.at[:, lanes(chip)], dst.at[rows(me)], relay_kv.at[t, me], recv_kv.at[t, me], other
        ).start()
    for h in (0, 1):
        for step in PARTNERS:
            dev = partner(step)
            for t, (src, dst) in enumerate(qd):
                remote(
                    src.at[:, lanes(dev * 2 + h)],
                    dst.at[h, rows(me)],
                    send_q.at[t, h, dev],
                    recv_q.at[t, h, me],
                    dev,
                ).start()
        for t, (src, dst) in enumerate(qd):
            pltpu.make_async_copy(src.at[:, lanes(me * 2 + h)], dst.at[h, rows(me)], recv_q.at[t, h, me]).start()

    dka[...] = jnp.zeros_like(dka)
    dva[...] = jnp.zeros_like(dva)

    def landed(t, dev):
        dst = kv[t][1]
        remote(dst.at[rows(dev)], dst.at[rows(dev)], relay_kv.at[t, dev], recv_kv.at[t, dev], other).wait_recv()

    def take(dev):
        kt[:, lanes(dev)] = kb[rows(dev), :].T

    def relay(i, carry):
        dev = ((chip + 7 - i) % 8) * 2 + core
        for t in (0, 1):
            landed(t, dev)

        @pl.when(dev != me)
        def _():
            for t in (0, 1):
                dst = kv[t][1]
                remote(
                    dst.at[rows(dev)], dst.at[rows(dev)], relay_kv.at[t, dev], recv_kv.at[t, dev], other
                ).start()

        take(dev)
        return carry

    lax.fori_loop(0, 8, relay, 0)

    def from_other(i, carry):
        dev = ((chip + 7 - i) % 8) * 2 + 1 - core
        for t in (0, 1):
            landed(t, dev)
        take(dev)
        return carry

    lax.fori_loop(0, 8, from_other, 0)

    def attend(h, rb, chunks, question):
        here = rows(rb, BLK)
        for dev in (rb * 2, rb * 2 + 1):
            for t in (0, 1):
                dst = qd[t][1]
                remote(
                    dst.at[h, rows(dev)], dst.at[h, rows(dev)], send_q.at[t, h, dev], recv_q.at[t, h, dev], other
                ).wait_recv()
        query = qb[h, here, :]
        grad = dob[h, here, :]
        i_pos = rb * BLK + lax.broadcasted_iota(jnp.int32, (1, BLK), 1)
        first = jnp.zeros((1, BLK), jnp.int32)
        if question:
            end = jnp.int32(DOC)
            first = first + DOC
            for c in range(NQ - 1):
                end = end + lens[c]
                first = jnp.where(i_pos >= end, end, first)
        peak = None
        for t, (chunk, masked) in enumerate(chunks):
            keys = rows(chunk, BLK)
            score = dot_t(kb[keys, :], query)
            if masked:
                j_pos = chunk * BLK + lax.broadcasted_iota(jnp.int32, (BLK, BLK), 0)
                seen = j_pos <= i_pos
                if question:
                    seen = seen & (j_pos >= first)
                score = jnp.where(seen, score, MASKED)
            s_buf[pl.ds(t * BLK, BLK), :] = score
            dp_buf[pl.ds(t * BLK, BLK), :] = dot_t(vb[keys, :], grad)
            top = fold(score, jnp.max)
            peak = top if peak is None else jnp.maximum(peak, top)
        peak = jnp.max(peak, axis=0, keepdims=True)
        total = jnp.zeros((8, BLK), F32)
        weighted = jnp.zeros((8, BLK), F32)
        for t in range(len(chunks)):
            at = pl.ds(t * BLK, BLK)
            prob = jnp.exp2((s_buf[at, :] - peak) * to_log2)
            s_buf[at, :] = prob
            total = total + fold(prob, jnp.sum)
            weighted = weighted + fold(prob * dp_buf[at, :], jnp.sum)
        inverse = 1.0 / jnp.sum(total, axis=0, keepdims=True)
        delta = jnp.sum(weighted, axis=0, keepdims=True) * inverse
        dq_t = jnp.zeros((HD, BLK), F32)
        for t, (chunk, _) in enumerate(chunks):
            at = pl.ds(t * BLK, BLK)
            keys = rows(chunk, BLK)
            prob = s_buf[at, :] * inverse
            score_grad = (prob * (dp_buf[at, :] - delta)).astype(BF)
            dva[keys, :] += dot_n(prob.astype(BF), grad)
            dka[keys, :] += dot_n(score_grad, query)
            dq_t = dq_t + dot_n(kt[:, lanes(chunk, BLK)], score_grad)
        dqb[h, here, :] = (dq_t * scaling).T.astype(BF)
        for dev in (rb * 2, rb * 2 + 1):
            src = dqb.at[h, rows(dev)]
            dst = dq_out.at[:, lanes(me * 2 + h)]

            @pl.when(dev == me)
            def _(src=src, dst=dst):
                pltpu.make_async_copy(src, dst, recv_dq.at[h, me]).start()

            @pl.when(dev != me)
            def _(src=src, dst=dst, dev=dev):
                remote(src, dst, send_dq.at[h, dev], recv_dq.at[h, me], dev).start()

    acc = (dka, dva)
    outs = (dk_out, dv_out)

    def part_copy(t, rb):
        return remote(
            acc[t].at[rows(rb * 2 + 1 - core)], part.at[rb, t], send_part.at[t, rb], recv_part.at[t, rb], other
        )

    def finish(rb):
        dev = rb * 2 + core
        for t in (0, 1):
            part_copy(t, rb).wait_recv()
            both = acc[t][rows(dev), :] + part[rb, t]
            if t == 0:
                both = both * scaling
            fin[rb, t] = both.astype(BF)
        for t in (0, 1):
            src = fin.at[rb, t]
            dst = outs[t].at[:, lanes(chip)]

            @pl.when(dev == me)
            def _(src=src, dst=dst, t=t):
                pltpu.make_async_copy(src, dst, recv_fin.at[t, chip]).start()

            @pl.when(dev != me)
            def _(src=src, dst=dst, t=t):
                remote(src, dst, send_fin.at[t, rb], recv_fin.at[t, chip], dev).start()

    def head(h, carry):
        def question_rows(i, c):
            rb = 7 - i
            chunks = [(n, False) for n in range(4)] + [(rb - 2 + n, True) for n in range(3)]
            attend(h, rb, chunks, True)

            @pl.when(h == 1)
            def _():
                for t in (0, 1):
                    part_copy(t, rb).start()

                @pl.when(i > 0)
                def _():
                    finish(rb + 1)

            return c

        lax.fori_loop(0, 4, question_rows, 0)
        for rb in (3, 2, 1, 0):
            attend(h, rb, [(n, n == rb) for n in range(rb + 1)], False)

            @pl.when(h == 1)
            def _(rb=rb):
                for t in (0, 1):
                    part_copy(t, rb).start()
                finish(rb + 1)

        return carry

    lax.fori_loop(0, 2, head, 0)
    finish(0)

    for step in PARTNERS:
        dev = partner(step)
        for t, (src, dst) in enumerate(qd):
            for h in (0, 1):
                remote(
                    src.at[:, lanes(dev * 2 + h)], dst.at[h, rows(me)], send_q.at[t, h, dev], recv_q.at[t, h, me], dev
                ).wait_send()
        for h in (0, 1):
            remote(
                dqb.at[h, rows(dev)], dq_out.at[:, lanes(dev * 2 + h)], send_dq.at[h, dev], recv_dq.at[h, dev], dev
            ).wait()
        if step[2] == 0:
            for t, (src, dst) in enumerate(kv):
                remote(
                    src.at[:, lanes(dev // 2)], dst.at[rows(me)], send_kv.at[t, dev], recv_kv.at[t, me], dev
                ).wait_send()
                remote(
                    dst.at[rows(dev)], dst.at[rows(dev)], relay_kv.at[t, dev], recv_kv.at[t, dev], other
                ).wait_send()
                remote(
                    fin.at[dev // 2, t],
                    outs[t].at[:, lanes(dev // 2)],
                    send_fin.at[t, dev // 2],
                    recv_fin.at[t, dev // 2],
                    dev,
                ).wait()
    for h in (0, 1):
        pltpu.make_async_copy(
            dqb.at[h, rows(me)], dq_out.at[:, lanes(me * 2 + h)], recv_dq.at[h, me]
        ).wait()
    for t, (src, dst) in enumerate(kv):
        remote(
            src.at[:, lanes(chip)], dst.at[rows(me)], relay_kv.at[t, me], recv_kv.at[t, me], other
        ).wait_send()
        pltpu.make_async_copy(fin.at[chip, t], outs[t].at[:, lanes(chip)], recv_fin.at[t, chip]).wait()
        for rb in range(8):
            part_copy(t, rb).wait_send()


def on_device(query_rows, key_rows, value_rows, out_grad, question_lengths):
    any_space = pl.BlockSpec(memory_space=pl.ANY)
    dma = pltpu.SemaphoreType.DMA
    return pl.pallas_call(
        kernel,
        name="exchange_attend",
        out_shape=(
            jax.ShapeDtypeStruct((TOK, QH * HD), BF),
            jax.ShapeDtypeStruct((TOK, KVH * HD), BF),
            jax.ShapeDtypeStruct((TOK, KVH * HD), BF),
        ),
        in_specs=[pl.BlockSpec(memory_space=pltpu.SMEM)] + [any_space] * 4,
        out_specs=(any_space,) * 3,
        scratch_shapes=[
            pltpu.VMEM((2, SEQ, HD), BF),
            pltpu.VMEM((2, SEQ, HD), BF),
            pltpu.VMEM((SEQ, HD), BF),
            pltpu.VMEM((SEQ, HD), BF),
            pltpu.VMEM((HD, SEQ), BF),
            pltpu.VMEM((7 * BLK, BLK), F32),
            pltpu.VMEM((7 * BLK, BLK), F32),
            pltpu.VMEM((SEQ, HD), F32),
            pltpu.VMEM((SEQ, HD), F32),
            pltpu.VMEM((2, SEQ, HD), BF),
            pltpu.VMEM((8, 2, TOK, HD), F32),
            pltpu.VMEM((8, 2, TOK, HD), BF),
            dma((2, DEVS)),
            dma((2, DEVS)),
            dma((2, 2, DEVS)),
            dma((2, 2, DEVS)),
            dma((2, DEVS)),
            dma((2, DEVS)),
            dma((2, DEVS)),
            dma((2, 8)),
            dma((2, 8)),
            dma((2, 8)),
            dma((2, 8)),
        ],
        compiler_params=pltpu.CompilerParams(
            collective_id=0, has_side_effects=True, vmem_limit_bytes=48 * 1024 * 1024
        ),
    )(question_lengths, query_rows, key_rows, value_rows, out_grad)


def solution(mesh):
    spec = P(("grp", "sp"), None)
    return jax.shard_map(
        on_device,
        mesh=mesh,
        in_specs=(spec, spec, spec, spec, P("grp")),
        out_specs=(spec, spec, spec),
        check_vma=False,
    )
```

time: 227 us -> 75.7 us (0.33); the launches traced: 223 us -> 75.4 us
  waiting for transfers between devices: 71.7 us -> 0 us
  Pallas kernels: 0 us -> 67.4 us
  matrix products: 63.5 us -> 0 us
  starting transfers between devices: 39.2 us -> 0 us
  local copies, waits for them, and re-layouts: 30.7 us -> 7.37 us
  other arithmetic: 15.9 us -> 0 us
    all_to_all x7 -> x0, waiting for transfers between devices: 71.7 us -> none  [the longest x1 17 us: on_device(): lax.all_to_all(query_rows, 'sp', split_axis=1, concat_axis=0, tiled=True)]
    pallas_call x0 -> x1, Pallas kernels: none -> 67.4 us  [on_device(): pl.pallas_call(kernel, name='exchange_attend', out_shape=(jax.ShapeDtypeS...]
    dot_general x60 -> x0, matrix products: 63.5 us -> none  [the longest x10 21.3 us: backward_block(): jnp.einsum('bkgd,skd->kgbs', grad_block, value_block, preferred_element_t...]
    all_to_all x7 -> x0, starting transfers between devices: 39.2 us -> none  [the longest x1 8.44 us: on_device(): lax.all_to_all(widen(key_rows, copies), 'sp', split_axis=1, concat_axis=0...]
    unnamed x172 -> x13, local copies, waits for them, and re-layouts: 12.3 us -> 7.37 us
    all_to_all x3 -> x0, local copies, waits for them, and re-layouts: 4.64 us -> none  [the longest x1 2.3 us: on_device(): lax.all_to_all(out_grad, 'sp', split_axis=1, concat_axis=0, tiled=True)]
    another operation x8 -> x0, local copies, waits for them, and re-layouts: 4.61 us -> none
    reduce_sum x7 -> x0, other arithmetic: 4.42 us -> none  [the longest x4 2.96 us: on_device(): jnp.sum(jnp.exp(score - peak[..., None]), axis=3)]
  transfers between devices with their start and end apart: 7 -> 0, of which waited for: 6 -> 0; matrix products, arithmetic and copies ran while one was open for 16% -> 0% of each run, Pallas kernels for 0% -> 0%
where the time goes in v1:
time: 75.7 us; the launch traced here: 75.4 us
  Pallas kernels  67.4 us (89%)
  local copies, waits for them, and re-layouts  7.37 us (10%)
    pallas_call x1, Pallas kernels, on_device(): pl.pallas_call(kernel, name='exchange_attend', out_shape=(jax.ShapeDtypeS...  67.4 us
    unnamed x13, local copies, waits for them, and re-layouts  7.37 us

profile of v1, /device:TPU:1, one launch (start us, length us, event | category | flops | bytes accessed | tf_op | source)
XLA Modules:
  0.0 75.4 jit_solution(13054022915908443442)
XLA Ops:
  0.6 0.0 copy-start
  0.6 1.2 %copy-done = bf16[128,4096]{1,0:T(8,128)(2,1)S(1)} copy-done((bf16[128,4096]{1,0:T(8,128)(2,1)S(1)}, bf16[128,4096]{1,0:T(8,128)(2,1)}, u32[]{:S(2)}) %copy-start) | copy-done | bytes 1048600
  1.9 0.0 copy-start.1
  1.9 1.2 %copy-done.1 = bf16[128,4096]{1,0:T(8,128)(2,1)S(1)} copy-done((bf16[128,4096]{1,0:T(8,128)(2,1)S(1)}, bf16[128,4096]{1,0:T(8,128)(2,1)}, u32[]{:S(2)}) %copy-start.1) | copy-done | bytes 1048600
  3.1 0.0 copy-start.2
  3.1 0.9 %copy-done.2 = bf16[128,1024]{1,0:T(8,128)(2,1)S(1)} copy-done((bf16[128,1024]{1,0:T(8,128)(2,1)S(1)}, bf16[128,1024]{1,0:T(8,128)(2,1)}, u32[]{:S(2)}) %copy-start.2) | copy-done | bytes 262168
  4.0 0.0 copy-start.3
  4.0 0.9 %copy-done.3 = bf16[128,1024]{1,0:T(8,128)(2,1)S(1)} copy-done((bf16[128,1024]{1,0:T(8,128)(2,1)S(1)}, bf16[128,1024]{1,0:T(8,128)(2,1)}, u32[]{:S(2)}) %copy-start.3) | copy-done | bytes 262168
  5.0 0.0 copy-start.4
  5.0 0.7 copy-done.4
  5.6 67.4 %exchange_attend.1 = (bf16[128,4096]{1,0:T(8,128)(2,1)S(1)}, bf16[128,1024]{1,0:T(8,128)(2,1)S(1)}, bf16[128,1024]{1,0:T(8,128)(2,1)S(1)}) custom-call(s32[8]{0:T(128)S(1)} %copy-done.4, bf16[128,4096]{1,0:T(8,128)(2,1)S(1)} %copy-done, bf16[128,1024]{1,0:T(8,128)(2,1)S(1)} %copy-done.2, bf16[128,1024]{1,0:T(8,128)(2,1)S(1)} %copy-done.3, ...), custom_call_target="tpu_custom_call" | custom-call | tf_op jit(solution)/shard_map/exchange_attend/pallas_call | solution.py:341
  73.1 1.0 %copy.11 = bf16[128,4096]{1,0:T(8,128)(2,1)} copy(bf16[128,4096]{1,0:T(8,128)(2,1)S(1)} %get-tuple-element.6) | data formatting | bytes 2097152
  74.0 0.7 copy.12
  74.7 0.7 copy.13
Async XLA Ops:
  0.6 1.2 %copy-start = (bf16[128,4096]{1,0:T(8,128)(2,1)S(1)}, bf16[128,4096]{1,0:T(8,128)(2,1)}, u32[]{:S(2)}) copy-start(bf16[128,4096]{1,0:T(8,128)(2,1)} %q_hbm.1) | copy-start | bytes 3145732
  1.9 1.2 %copy-start.1 = (bf16[128,4096]{1,0:T(8,128)(2,1)S(1)}, bf16[128,4096]{1,0:T(8,128)(2,1)}, u32[]{:S(2)}) copy-start(bf16[128,4096]{1,0:T(8,128)(2,1)} %do_hbm.1) | copy-start | bytes 3145732
  3.1 0.9 %copy-start.2 = (bf16[128,1024]{1,0:T(8,128)(2,1)S(1)}, bf16[128,1024]{1,0:T(8,128)(2,1)}, u32[]{:S(2)}) copy-start(bf16[128,1024]{1,0:T(8,128)(2,1)} %k_hbm.1) | copy-start | bytes 786436
  4.0 0.9 %copy-start.3 = (bf16[128,1024]{1,0:T(8,128)(2,1)S(1)}, bf16[128,1024]{1,0:T(8,128)(2,1)}, u32[]{:S(2)}) copy-start(bf16[128,1024]{1,0:T(8,128)(2,1)} %v_hbm.1) | copy-start | bytes 786436
  5.0 0.7 copy-start.4

commit v2 on v1

v2 whole, which is shorter than its diff:
```python
import functools
import math

import jax
import jax.numpy as jnp
from jax import lax
from jax.experimental import pallas as pl
from jax.experimental.pallas import tpu as pltpu
from jax.sharding import PartitionSpec as P

HD = 128
QH = 32
KVH = 8
SEQ = 2048
DOC = 1024
NQ = 8
TOK = 128
HALF = 64
BLK = 256
DEVS = 16
MASKED = -1e30
MESH = pl.DeviceIdType.MESH
BF = jnp.bfloat16
F32 = jnp.float32

PARTNERS = tuple(
    (a, b, c)
    for c in (0, 1)
    for a, b in ((1, 2), (1, 1), (0, 2), (1, 3), (1, 0), (0, 1), (0, 3), (0, 0))
    if (a, b, c) != (0, 0, 0)
)


def dot_t(a, b):
    return lax.dot_general(a, b, (((1,), (1,)), ((), ())), preferred_element_type=F32)


def dot_n(a, b):
    return lax.dot_general(a, b, (((1,), (0,)), ((), ())), preferred_element_type=F32)


def fold(x, op):
    return op(x.reshape(x.shape[0] // 8, 8, x.shape[1]), axis=0)


def kernel(
    lens,
    q_hbm,
    k_hbm,
    v_hbm,
    do_hbm,
    dq_out,
    dk_out,
    dv_out,
    qd,
    kb,
    vb,
    kt,
    s_buf,
    dp_buf,
    dka,
    dva,
    dqb,
    part,
    fin,
    send_kv,
    recv_kv,
    relay_kv,
    send_q,
    recv_q,
    send_dq,
    recv_dq,
    send_part,
    recv_part,
    send_fin,
    recv_fin,
):
    grp = lax.axis_index("grp")
    me = lax.axis_index("sp")
    far = me // 8
    yy = (me // 2) % 4
    core = me % 2
    chip = me // 2
    other = chip * 2 + 1 - core
    scaling = 1.0 / math.sqrt(HD)
    to_log2 = scaling * math.log2(math.e)

    def partner(step):
        a, b, c = step
        return ((far + a) % 2) * 8 + ((yy + b) % 4) * 2 + (core + c) % 2

    def lanes(index, width=HD):
        return pl.ds(pl.multiple_of(index * width, width), width)

    def rows(index, width=TOK):
        return pl.ds(pl.multiple_of(index * width, width), width)

    def remote(src, dst, ss, rs, dev):
        return pltpu.make_async_remote_copy(
            src_ref=src, dst_ref=dst, send_sem=ss, recv_sem=rs, device_id=(grp, dev), device_id_type=MESH
        )

    def local(src, dst, sem):
        return pltpu.make_async_copy(src, dst, sem)

    barrier = pltpu.get_barrier_semaphore()
    for step in PARTNERS:
        pl.semaphore_signal(barrier, inc=1, device_id=(grp, partner(step)), device_id_type=MESH)
    pl.semaphore_wait(barrier, len(PARTNERS))

    kv = ((k_hbm, kb), (v_hbm, vb))
    qs = (q_hbm, do_hbm)

    for step in PARTNERS:
        if step[2] == 0:
            dev = partner(step)
            for t, (src, dst) in enumerate(kv):
                remote(src.at[:, lanes(dev // 2)], dst.at[rows(me)], send_kv.at[t], recv_kv.at[t, me], dev).start()
    for t, (src, dst) in enumerate(kv):
        local(src.at[:, lanes(chip)], dst.at[rows(me)], recv_kv.at[t, me]).start()
        remote(src.at[:, lanes(chip)], dst.at[rows(me)], relay_kv.at[t], recv_kv.at[t, me], other).start()
    for h in (0, 1):
        for half in (0, 1):
            top = pl.ds(half * HALF, HALF)
            for step in PARTNERS:
                dev = partner(step)
                for t, src in enumerate(qs):
                    remote(
                        src.at[top, lanes(dev * 2 + h)],
                        qd.at[h, half, me, t],
                        send_q.at[t],
                        recv_q.at[h, half, me // 4],
                        dev,
                    ).start()
            for t, src in enumerate(qs):
                local(src.at[top, lanes(me * 2 + h)], qd.at[h, half, me, t], recv_q.at[h, half, me // 4]).start()

    dka[...] = jnp.zeros_like(dka)
    dva[...] = jnp.zeros_like(dva)

    def take(dev, pass_on):
        for t, (_, dst) in enumerate(kv):
            remote(dst.at[rows(dev)], dst.at[rows(dev)], relay_kv.at[t], recv_kv.at[t, dev], other).wait_recv()
        if pass_on:

            @pl.when(dev != me)
            def _():
                for t, (_, dst) in enumerate(kv):
                    remote(dst.at[rows(dev)], dst.at[rows(dev)], relay_kv.at[t], recv_kv.at[t, dev], other).start()

        kt[:, lanes(dev)] = kb[rows(dev), :].T

    def from_far(i, carry):
        take(((chip + 7 - i) % 8) * 2 + core, True)
        return carry

    def from_other(i, carry):
        take(((chip + 7 - i) % 8) * 2 + 1 - core, False)
        return carry

    lax.fori_loop(0, 8, from_far, 0)
    lax.fori_loop(0, 8, from_other, 0)

    def attend(h, half, span, chunks, question):
        four = pl.ds(span * 4, 4)
        local(qd.at[h, half, four], qd.at[h, half, four], recv_q.at[h, half, span]).wait()
        query = qd[h, half, four, 0].reshape(BLK, HD)
        grad = qd[h, half, four, 1].reshape(BLK, HD)
        lane = lax.broadcasted_iota(jnp.int32, (1, BLK), 1)
        i_pos = span * (4 * TOK) + half * HALF + lane + (lane >> 6) * (TOK - HALF)
        first = jnp.zeros((1, BLK), jnp.int32)
        if question:
            end = jnp.int32(DOC)
            first = first + DOC
            for c in range(NQ - 1):
                end = end + lens[c]
                first = jnp.where(i_pos >= end, end, first)
        peak = None
        for t, (chunk, masked) in enumerate(chunks):
            keys = rows(chunk, BLK)
            score = dot_t(kb[keys, :], query)
            if masked:
                j_pos = chunk * BLK + lax.broadcasted_iota(jnp.int32, (BLK, BLK), 0)
                seen = j_pos <= i_pos
                if question:
                    seen = seen & (j_pos >= first)
                score = jnp.where(seen, score, MASKED)
            s_buf[pl.ds(t * BLK, BLK), :] = score
            dp_buf[pl.ds(t * BLK, BLK), :] = dot_t(vb[keys, :], grad)
            top = fold(score, jnp.max)
            peak = top if peak is None else jnp.maximum(peak, top)
        peak = jnp.max(peak, axis=0, keepdims=True)
        total = jnp.zeros((8, BLK), F32)
        weighted = jnp.zeros((8, BLK), F32)
        for t in range(len(chunks)):
            at = pl.ds(t * BLK, BLK)
            prob = jnp.exp2((s_buf[at, :] - peak) * to_log2)
            s_buf[at, :] = prob
            total = total + fold(prob, jnp.sum)
            weighted = weighted + fold(prob * dp_buf[at, :], jnp.sum)
        inverse = 1.0 / jnp.sum(total, axis=0, keepdims=True)
        delta = jnp.sum(weighted, axis=0, keepdims=True) * inverse
        dq_t = jnp.zeros((HD, BLK), F32)
        for t, (chunk, _) in enumerate(chunks):
            at = pl.ds(t * BLK, BLK)
            keys = rows(chunk, BLK)
            prob = s_buf[at, :] * inverse
            score_grad = (prob * (dp_buf[at, :] - delta)).astype(BF)
            dva[keys, :] += dot_n(prob.astype(BF), grad)
            dka[keys, :] += dot_n(score_grad, query)
            dq_t = dq_t + dot_n(kt[:, lanes(chunk, BLK)], score_grad)
        dqb[four, h, half] = (dq_t * scaling).T.astype(BF).reshape(4, HALF, HD)

        def give(n, carry):
            dev = span * 4 + n
            src = dqb.at[dev, h, half]
            dst = dq_out.at[pl.ds(pl.multiple_of(half * HALF, HALF), HALF), lanes(me * 2 + h)]

            @pl.when(dev == me)
            def _():
                local(src, dst, recv_dq).start()

            @pl.when(dev != me)
            def _():
                remote(src, dst, send_dq, recv_dq, dev).start()

            return carry

        lax.fori_loop(0, 4, give, 0)

    acc = (dka, dva)
    outs = (dk_out, dv_out)

    def share(rb):
        for t in (0, 1):
            remote(acc[t].at[rows(rb * 2 + 1 - core)], part.at[rb, t], send_part, recv_part.at[rb], other).start()

    def close(rb):
        dev = rb * 2 + core
        local(part.at[rb], part.at[rb], recv_part.at[rb]).wait()
        for t in (0, 1):
            both = acc[t][rows(dev), :] + part[rb, t]
            if t == 0:
                both = both * scaling
            fin[rb, t] = both.astype(BF)
        for t in (0, 1):
            src = fin.at[rb, t]
            dst = outs[t].at[:, lanes(chip)]

            @pl.when(dev == me)
            def _(src=src, dst=dst, t=t):
                local(src, dst, recv_fin.at[t]).start()

            @pl.when(dev != me)
            def _(src=src, dst=dst, t=t):
                remote(src, dst, send_fin, recv_fin.at[t], dev).start()

    def chunk_step(n, carry):
        h = n // 2
        half = n % 2
        last = n // 3

        def span_step(i, c):
            span = last * (3 - i) + (1 - last) * ((chip // 2 + 1 + i) % 4)

            @pl.when(span >= 2)
            def _():
                chunks = [(m, False) for m in range(4)] + [(span * 2 - 2 + m, True) for m in range(4)]
                attend(h, half, span, chunks, True)

            for doc in (0, 1):

                @pl.when(span == doc)
                def _(doc=doc):
                    attend(h, half, doc, [(m, m >= doc * 2) for m in range(doc * 2 + 2)], False)

            @pl.when(last == 1)
            def _():
                share(span * 2)
                share(span * 2 + 1)

                @pl.when(i > 0)
                def _():
                    close(span * 2 + 2)
                    close(span * 2 + 3)

            return c

        lax.fori_loop(0, 4, span_step, 0)
        return carry

    lax.fori_loop(0, 4, chunk_step, 0)
    close(0)
    close(1)

    for t, (src, _) in enumerate(kv):
        local(src.at[:, pl.ds(0, 7 * HD)], src.at[:, pl.ds(0, 7 * HD)], send_kv.at[t]).wait()
        local(src, src, relay_kv.at[t]).wait()
    for t, src in enumerate(qs):
        local(src.at[:, pl.ds(0, 30 * HD)], src.at[:, pl.ds(0, 30 * HD)], send_q.at[t]).wait()
    local(part, part, send_part).wait()
    local(dqb.at[pl.ds(0, 15)], dqb.at[pl.ds(0, 15)], send_dq).wait()
    local(fin.at[pl.ds(0, 7)], fin.at[pl.ds(0, 7)], send_fin).wait()
    local(dq_out, dq_out, recv_dq).wait()
    for t in (0, 1):
        local(outs[t], outs[t], recv_fin.at[t]).wait()


def put(dq, dk, dv, dq_out, dk_out, dv_out, sems):
    copies = [
        pltpu.make_async_copy(src, dst, sems.at[n])
        for n, (src, dst) in enumerate(((dq, dq_out), (dk, dk_out), (dv, dv_out)))
    ]
    for copy in copies:
        copy.start()
    for copy in copies:
        copy.wait()


def on_device(query_rows, key_rows, value_rows, out_grad, question_lengths):
    hbm = pl.BlockSpec(memory_space=pltpu.HBM)
    any_space = pl.BlockSpec(memory_space=pl.ANY)
    dma = pltpu.SemaphoreType.DMA
    grads = pl.pallas_call(
        kernel,
        name="exchange_attend",
        out_shape=(
            pltpu.VMEM((TOK, QH * HD), BF),
            pltpu.VMEM((TOK, KVH * HD), BF),
            pltpu.VMEM((TOK, KVH * HD), BF),
        ),
        in_specs=[pl.BlockSpec(memory_space=pltpu.SMEM)] + [hbm] * 4,
        out_specs=(any_space,) * 3,
        scratch_shapes=[
            pltpu.VMEM((2, 2, DEVS, 2, HALF, HD), BF),
            pltpu.VMEM((SEQ, HD), BF),
            pltpu.VMEM((SEQ, HD), BF),
            pltpu.VMEM((HD, SEQ), BF),
            pltpu.VMEM((8 * BLK, BLK), F32),
            pltpu.VMEM((8 * BLK, BLK), F32),
            pltpu.VMEM((SEQ, HD), F32),
            pltpu.VMEM((SEQ, HD), F32),
            pltpu.VMEM((DEVS, 2, 2, HALF, HD), BF),
            pltpu.VMEM((8, 2, TOK, HD), F32),
            pltpu.VMEM((8, 2, TOK, HD), BF),
            dma((2,)),
            dma((2, DEVS)),
            dma((2,)),
            dma((2,)),
            dma((2, 2, 4)),
            dma,
            dma,
            dma,
            dma((8,)),
            dma,
            dma((2,)),
        ],
        compiler_params=pltpu.CompilerParams(
            collective_id=0, has_side_effects=True, vmem_limit_bytes=60 * 1024 * 1024
        ),
    )(question_lengths, query_rows, key_rows, value_rows, out_grad)
    return pl.pallas_call(
        put,
        name="put",
        out_shape=(
            jax.ShapeDtypeStruct((TOK, QH * HD), BF),
            jax.ShapeDtypeStruct((TOK, KVH * HD), BF),
            jax.ShapeDtypeStruct((TOK, KVH * HD), BF),
        ),
        in_specs=[any_space] * 3,
        out_specs=(any_space,) * 3,
        scratch_shapes=[dma((3,))],
    )(*(pltpu.with_memory_space_constraint(g, pltpu.VMEM) for g in grads))


def solution(mesh):
    spec = P(("grp", "sp"), None)
    return jax.shard_map(
        on_device,
        mesh=mesh,
        in_specs=(spec, spec, spec, spec, P("grp")),
        out_specs=(spec, spec, spec),
        check_vma=False,
    )
```

time: 75.7 us -> 63.2 us (0.83)
  local copies, waits for them, and re-layouts: 7.37 us -> 0 us
  Pallas kernels: 67.4 us -> 62.4 us
    unnamed x13 -> x0, local copies, waits for them, and re-layouts: 7.37 us -> none
    pallas_call x1 -> x2, Pallas kernels: 67.4 us -> 62.4 us  [the longest x1 61.3 us: on_device(): pl.pallas_call(kernel, name='exchange_attend', out_shape=(pltpu.VMEM((TOK...]
where the time goes in v2:
time: 63.2 us; the launch traced here: 63.1 us
  Pallas kernels  62.4 us (99%)
  between operations  0.64 us (1%)
    pallas_call x1, Pallas kernels, on_device(): pl.pallas_call(kernel, name='exchange_attend', out_shape=(pltpu.VMEM((TOK...  61.3 us

profile of v2, /device:TPU:1, one launch (start us, length us, event | category | flops | bytes accessed | tf_op | source)
XLA Modules:
  0.0 63.1 jit_solution(17770790377674483596)
XLA Ops:
  0.6 61.3 %exchange_attend.1 = (bf16[128,4096]{1,0:T(8,128)(2,1)S(1)}, bf16[128,1024]{1,0:T(8,128)(2,1)S(1)}, bf16[128,1024]{1,0:T(8,128)(2,1)S(1)}) custom-call(s32[8]{0:T(128)} %lens.1, bf16[128,4096]{1,0:T(8,128)(2,1)} %q_hbm.1, bf16[128,1024]{1,0:T(8,128)(2,1)} %k_hbm.1, bf16[128,1024]{1,0:T(8,128)(2,1)} %v_hbm.1, bf16[128,4096]{1,0:T(8,128)(2,1)} %do_hbm.1), custom_call_target="tpu_custom_call" | custom-call | tf_op jit(solution)/shard_map/exchange_attend/pallas_call | solution.py:324
  61.9 1.2 %put.1 = (bf16[128,4096]{1,0:T(8,128)(2,1)}, bf16[128,1024]{1,0:T(8,128)(2,1)}, bf16[128,1024]{1,0:T(8,128)(2,1)}) custom-call(bf16[128,4096]{1,0:T(8,128)(2,1)S(1)} %get-tuple-element.6.dq, bf16[128,1024]{1,0:T(8,128)(2,1)S(1)} %get-tuple-element.7.dk, bf16[128,1024]{1,0:T(8,128)(2,1)S(1)} %get-tuple-element.8.dv), custom_call_target="tpu_custom_call" | custom-call | tf_op jit(solution)/shard_map/put/pallas_call | solution.py:362

commit v3 on v2

--- a/solution.py
+++ b/solution.py
@@ -18,6 +18,7 @@
 HALF = 64
 BLK = 256
 DEVS = 16
+STRIP = 64
 MASKED = -1e30
 MESH = pl.DeviceIdType.MESH
 BF = jnp.bfloat16
@@ -106,6 +107,8 @@
     barrier = pltpu.get_barrier_semaphore()
     for step in PARTNERS:
         pl.semaphore_signal(barrier, inc=1, device_id=(grp, partner(step)), device_id_type=MESH)
+    dka[...] = jnp.zeros_like(dka)
+    dva[...] = jnp.zeros_like(dva)
     pl.semaphore_wait(barrier, len(PARTNERS))
 
     kv = ((k_hbm, kb), (v_hbm, vb))
@@ -135,9 +138,6 @@
             for t, src in enumerate(qs):
                 local(src.at[top, lanes(me * 2 + h)], qd.at[h, half, me, t], recv_q.at[h, half, me // 4]).start()
 
-    dka[...] = jnp.zeros_like(dka)
-    dva[...] = jnp.zeros_like(dva)
-
     def take(dev, pass_on):
         for t, (_, dst) in enumerate(kv):
             remote(dst.at[rows(dev)], dst.at[rows(dev)], relay_kv.at[t], recv_kv.at[t, dev], other).wait_recv()
@@ -161,58 +161,81 @@
     lax.fori_loop(0, 8, from_far, 0)
     lax.fori_loop(0, 8, from_other, 0)
 
-    def attend(h, half, span, chunks, question):
+    def load(h, half, span, slot):
         four = pl.ds(span * 4, 4)
         local(qd.at[h, half, four], qd.at[h, half, four], recv_q.at[h, half, span]).wait()
-        query = qd[h, half, four, 0].reshape(BLK, HD)
-        grad = qd[h, half, four, 1].reshape(BLK, HD)
+        question = span >= 2
         lane = lax.broadcasted_iota(jnp.int32, (1, BLK), 1)
         i_pos = span * (4 * TOK) + half * HALF + lane + (lane >> 6) * (TOK - HALF)
-        first = jnp.zeros((1, BLK), jnp.int32)
+        first = None
         if question:
             end = jnp.int32(DOC)
-            first = first + DOC
+            first = jnp.full((1, BLK), DOC, jnp.int32)
             for c in range(NQ - 1):
                 end = end + lens[c]
                 first = jnp.where(i_pos >= end, end, first)
-        peak = None
-        for t, (chunk, masked) in enumerate(chunks):
-            keys = rows(chunk, BLK)
-            score = dot_t(kb[keys, :], query)
-            if masked:
-                j_pos = chunk * BLK + lax.broadcasted_iota(jnp.int32, (BLK, BLK), 0)
-                seen = j_pos <= i_pos
-                if question:
-                    seen = seen & (j_pos >= first)
-                score = jnp.where(seen, score, MASKED)
-            s_buf[pl.ds(t * BLK, BLK), :] = score
-            dp_buf[pl.ds(t * BLK, BLK), :] = dot_t(vb[keys, :], grad)
-            top = fold(score, jnp.max)
-            peak = top if peak is None else jnp.maximum(peak, top)
-        peak = jnp.max(peak, axis=0, keepdims=True)
-        total = jnp.zeros((8, BLK), F32)
-        weighted = jnp.zeros((8, BLK), F32)
-        for t in range(len(chunks)):
-            at = pl.ds(t * BLK, BLK)
-            prob = jnp.exp2((s_buf[at, :] - peak) * to_log2)
+        return dict(
+            query=qd[h, half, four, 0].reshape(BLK, HD),
+            grad=qd[h, half, four, 1].reshape(BLK, HD),
+            i_pos=i_pos,
+            first=first,
+            tiles=span * 2 + 2,
+            base=slot,
+            span=span,
+            dq=jnp.zeros((HD, BLK), F32),
+            peak=None,
+            total=jnp.zeros((8, BLK), F32),
+            weighted=jnp.zeros((8, BLK), F32),
+        )
+
+    def score_tile(w, t):
+        keys = pl.ds(t * BLK, BLK)
+        score = dot_t(kb[keys, :], w["query"])
+        if t >= (4 if w["first"] is not None else w["span"] * 2):
+            j_pos = t * BLK + lax.broadcasted_iota(jnp.int32, (BLK, BLK), 0)
+            seen = j_pos <= w["i_pos"]
+            if w["first"] is not None:
+                seen = seen & (j_pos >= w["first"])
+            score = jnp.where(seen, score, MASKED)
+        at = pl.ds((w["base"] + t) * BLK, BLK)
+        s_buf[at, :] = score
+        dp_buf[at, :] = dot_t(vb[keys, :], w["grad"])
+        top = fold(score, jnp.max)
+        w["peak"] = top if w["peak"] is None else jnp.maximum(w["peak"], top)
+
+    def prob_tile(w, t):
+        if t == 0:
+            w["peak"] = jnp.max(w["peak"], axis=0, keepdims=True)
+        for u in range(BLK // STRIP):
+            at = pl.ds((w["base"] + t) * BLK + u * STRIP, STRIP)
+            prob = jnp.exp2((s_buf[at, :] - w["peak"]) * to_log2)
             s_buf[at, :] = prob
-            total = total + fold(prob, jnp.sum)
-            weighted = weighted + fold(prob * dp_buf[at, :], jnp.sum)
-        inverse = 1.0 / jnp.sum(total, axis=0, keepdims=True)
-        delta = jnp.sum(weighted, axis=0, keepdims=True) * inverse
-        dq_t = jnp.zeros((HD, BLK), F32)
-        for t, (chunk, _) in enumerate(chunks):
-            at = pl.ds(t * BLK, BLK)
-            keys = rows(chunk, BLK)
-            prob = s_buf[at, :] * inverse
-            score_grad = (prob * (dp_buf[at, :] - delta)).astype(BF)
-            dva[keys, :] += dot_n(prob.astype(BF), grad)
-            dka[keys, :] += dot_n(score_grad, query)
-            dq_t = dq_t + dot_n(kt[:, lanes(chunk, BLK)], score_grad)
-        dqb[four, h, half] = (dq_t * scaling).T.astype(BF).reshape(4, HALF, HD)
+            w["total"] = w["total"] + fold(prob, jnp.sum)
+            w["weighted"] = w["weighted"] + fold(prob * dp_buf[at, :], jnp.sum)
+
+    def grad_tile(w, t):
+        if t == 0:
+            w["inverse"] = 1.0 / jnp.sum(w["total"], axis=0, keepdims=True)
+            w["delta"] = jnp.sum(w["weighted"], axis=0, keepdims=True) * w["inverse"]
+        keys = pl.ds(t * BLK, BLK)
+        low = []
+        slopes = []
+        for u in range(BLK // STRIP):
+            at = pl.ds((w["base"] + t) * BLK + u * STRIP, STRIP)
+            prob = s_buf[at, :] * w["inverse"]
+            low.append(prob.astype(BF))
+            slopes.append((prob * (dp_buf[at, :] - w["delta"])).astype(BF))
+        score_grad = jnp.concatenate(slopes, axis=0)
+        dva[keys, :] += dot_n(jnp.concatenate(low, axis=0), w["grad"])
+        dka[keys, :] += dot_n(score_grad, w["query"])
+        w["dq"] = w["dq"] + dot_n(kt[:, keys], score_grad)
+
+    def give_back(h, half, w):
+        span = w["span"]
+        dqb[pl.ds(span * 4, 4), h, half] = (w["dq"] * scaling).T.astype(BF).reshape(4, HALF, HD)
 
         def give(n, carry):
-            dev = span * 4 + n
+            dev = span * 4 + (n + chip) % 4
             src = dqb.at[dev, h, half]
             dst = dq_out.at[pl.ds(pl.multiple_of(half * HALF, HALF), HALF), lanes(me * 2 + h)]
 
@@ -227,6 +250,16 @@
             return carry
 
         lax.fori_loop(0, 4, give, 0)
+
+    def attend(h, half, ask, doc):
+        a = load(h, half, ask, 0)
+        b = load(h, half, doc, ask * 2 + 2)
+        for phase in (score_tile, prob_tile, grad_tile):
+            for w in (b, a):
+                for t in range(w["tiles"]):
+                    phase(w, t)
+                if phase is grad_tile:
+                    give_back(h, half, w)
 
     acc = (dka, dva)
     outs = (dk_out, dv_out)
@@ -258,40 +291,31 @@
     def chunk_step(n, carry):
         h = n // 2
         half = n % 2
-        last = n // 3
-
-        def span_step(i, c):
-            span = last * (3 - i) + (1 - last) * ((chip // 2 + 1 + i) % 4)
-
-            @pl.when(span >= 2)
-            def _():
-                chunks = [(m, False) for m in range(4)] + [(span * 2 - 2 + m, True) for m in range(4)]
-                attend(h, half, span, chunks, True)
-
-            for doc in (0, 1):
-
-                @pl.when(span == doc)
-                def _(doc=doc):
-                    attend(h, half, doc, [(m, m >= doc * 2) for m in range(doc * 2 + 2)], False)
-
-            @pl.when(last == 1)
-            def _():
-                share(span * 2)
-                share(span * 2 + 1)
-
-                @pl.when(i > 0)
-                def _():
-                    close(span * 2 + 2)
-                    close(span * 2 + 3)
+
+        def pair_step(i, c):
+            for pair in (0, 1):
+
+                @pl.when((chip // 2 + i) % 2 == pair)
+                def _(pair=pair):
+                    attend(h, half, 3 - pair, pair)
 
             return c
 
-        lax.fori_loop(0, 4, span_step, 0)
+        lax.fori_loop(0, 2, pair_step, 0)
         return carry
 
     lax.fori_loop(0, 4, chunk_step, 0)
-    close(0)
-    close(1)
+
+    def share_step(i, carry):
+        share((chip + 1 + i) % 8)
+        return carry
+
+    def close_step(i, carry):
+        close((chip + 1 + i) % 8)
+        return carry
+
+    lax.fori_loop(0, 8, share_step, 0)
+    lax.fori_loop(0, 8, close_step, 0)
 
     for t, (src, _) in enumerate(kv):
         local(src.at[:, pl.ds(0, 7 * HD)], src.at[:, pl.ds(0, 7 * HD)], send_kv.at[t]).wait()
@@ -307,10 +331,8 @@
 
 
 def put(dq, dk, dv, dq_out, dk_out, dv_out, sems):
-    copies = [
-        pltpu.make_async_copy(src, dst, sems.at[n])
-        for n, (src, dst) in enumerate(((dq, dq_out), (dk, dk_out), (dv, dv_out)))
-    ]
+    pieces = ((dq, dq_out), (dk, dk_out), (dv, dv_out))
+    copies = [pltpu.make_async_copy(src, dst, sems.at[n]) for n, (src, dst) in enumerate(pieces)]
     for copy in copies:
         copy.start()
     for copy in copies:
@@ -336,8 +358,8 @@
             pltpu.VMEM((SEQ, HD), BF),
             pltpu.VMEM((SEQ, HD), BF),
             pltpu.VMEM((HD, SEQ), BF),
-            pltpu.VMEM((8 * BLK, BLK), F32),
-            pltpu.VMEM((8 * BLK, BLK), F32),
+            pltpu.VMEM((10 * BLK, BLK), F32),
+            pltpu.VMEM((10 * BLK, BLK), F32),
             pltpu.VMEM((SEQ, HD), F32),
             pltpu.VMEM((SEQ, HD), F32),
             pltpu.VMEM((DEVS, 2, 2, HALF, HD), BF),

time: 63.2 us -> 58.3 us (0.922)
  Pallas kernels: 62.4 us -> 57.6 us
    pallas_call x1, Pallas kernels: 61.3 us -> 56.5 us  [on_device(): pl.pallas_call(kernel, name='exchange_attend', out_shape=(pltpu.VMEM((TOK...]
where the time goes in v3:
time: 58.3 us
  Pallas kernels  57.6 us (99%)
  between operations  0.64 us (1%)
    pallas_call x1, Pallas kernels, on_device(): pl.pallas_call(kernel, name='exchange_attend', out_shape=(pltpu.VMEM((TOK...  56.5 us

profile of v3, /device:TPU:1, one launch (start us, length us, event | category | flops | bytes accessed | tf_op | source)
XLA Modules:
  0.0 58.3 jit_solution(2521108652009973906)
XLA Ops:
  0.6 56.5 %exchange_attend.1 = (bf16[128,4096]{1,0:T(8,128)(2,1)S(1)}, bf16[128,1024]{1,0:T(8,128)(2,1)S(1)}, bf16[128,1024]{1,0:T(8,128)(2,1)S(1)}) custom-call(s32[8]{0:T(128)} %lens.1, bf16[128,4096]{1,0:T(8,128)(2,1)} %q_hbm.1, bf16[128,1024]{1,0:T(8,128)(2,1)} %k_hbm.1, bf16[128,1024]{1,0:T(8,128)(2,1)} %v_hbm.1, bf16[128,4096]{1,0:T(8,128)(2,1)} %do_hbm.1), custom_call_target="tpu_custom_call" | custom-call | tf_op jit(solution)/shard_map/exchange_attend/pallas_call | solution.py:346
  57.1 1.2 %put.1 = (bf16[128,4096]{1,0:T(8,128)(2,1)}, bf16[128,1024]{1,0:T(8,128)(2,1)}, bf16[128,1024]{1,0:T(8,128)(2,1)}) custom-call(bf16[128,4096]{1,0:T(8,128)(2,1)S(1)} %get-tuple-element.6.dq, bf16[128,1024]{1,0:T(8,128)(2,1)S(1)} %get-tuple-element.7.dk, bf16[128,1024]{1,0:T(8,128)(2,1)S(1)} %get-tuple-element.8.dv), custom_call_target="tpu_custom_call" | custom-call | tf_op jit(solution)/shard_map/put/pallas_call | solution.py:384

commit v4 on v3

--- a/solution.py
+++ b/solution.py
@@ -18,6 +18,7 @@
 HALF = 64
 BLK = 256
 DEVS = 16
+SPANS = ((3, 2), (1, 0))
 STRIP = 64
 MASKED = -1e30
 MESH = pl.DeviceIdType.MESH
@@ -27,7 +28,7 @@
 PARTNERS = tuple(
     (a, b, c)
     for c in (0, 1)
-    for a, b in ((1, 2), (1, 1), (0, 2), (1, 3), (1, 0), (0, 1), (0, 3), (0, 0))
+    for a, b in ((0, 0), (0, 1), (1, 0), (0, 3), (1, 2), (0, 2), (1, 1), (1, 3))
     if (a, b, c) != (0, 0, 0)
 )
 
@@ -46,13 +47,17 @@
 
 def kernel(
     lens,
-    q_hbm,
-    k_hbm,
-    v_hbm,
-    do_hbm,
+    q_in,
+    k_in,
+    v_in,
+    do_in,
     dq_out,
     dk_out,
     dv_out,
+    q_own,
+    k_own,
+    v_own,
+    do_own,
     qd,
     kb,
     vb,
@@ -75,6 +80,7 @@
     recv_part,
     send_fin,
     recv_fin,
+    staged,
 ):
     grp = lax.axis_index("grp")
     me = lax.axis_index("sp")
@@ -104,15 +110,23 @@
     def local(src, dst, sem):
         return pltpu.make_async_copy(src, dst, sem)
 
+    staging = [
+        local(src, dst, staged.at[n])
+        for n, (src, dst) in enumerate(((k_in, k_own), (v_in, v_own), (q_in, q_own), (do_in, do_own)))
+    ]
+    for copy in staging:
+        copy.start()
     barrier = pltpu.get_barrier_semaphore()
     for step in PARTNERS:
         pl.semaphore_signal(barrier, inc=1, device_id=(grp, partner(step)), device_id_type=MESH)
     dka[...] = jnp.zeros_like(dka)
     dva[...] = jnp.zeros_like(dva)
+    for copy in staging:
+        copy.wait()
     pl.semaphore_wait(barrier, len(PARTNERS))
 
-    kv = ((k_hbm, kb), (v_hbm, vb))
-    qs = (q_hbm, do_hbm)
+    kv = ((k_own, kb), (v_own, vb))
+    qs = (q_own, do_own)
 
     for step in PARTNERS:
         if step[2] == 0:
@@ -251,9 +265,9 @@
 
         lax.fori_loop(0, 4, give, 0)
 
-    def attend(h, half, ask, doc):
-        a = load(h, half, ask, 0)
-        b = load(h, half, doc, ask * 2 + 2)
+    def attend(h, half, later, earlier):
+        a = load(h, half, later, 0)
+        b = load(h, half, earlier, later * 2 + 2)
         for phase in (score_tile, prob_tile, grad_tile):
             for w in (b, a):
                 for t in range(w["tiles"]):
@@ -297,7 +311,7 @@
 
                 @pl.when((chip // 2 + i) % 2 == pair)
                 def _(pair=pair):
-                    attend(h, half, 3 - pair, pair)
+                    attend(h, half, *SPANS[pair])
 
             return c
 
@@ -354,12 +368,16 @@
         in_specs=[pl.BlockSpec(memory_space=pltpu.SMEM)] + [hbm] * 4,
         out_specs=(any_space,) * 3,
         scratch_shapes=[
+            pltpu.VMEM((TOK, QH * HD), BF),
+            pltpu.VMEM((TOK, KVH * HD), BF),
+            pltpu.VMEM((TOK, KVH * HD), BF),
+            pltpu.VMEM((TOK, QH * HD), BF),
             pltpu.VMEM((2, 2, DEVS, 2, HALF, HD), BF),
             pltpu.VMEM((SEQ, HD), BF),
             pltpu.VMEM((SEQ, HD), BF),
             pltpu.VMEM((HD, SEQ), BF),
-            pltpu.VMEM((10 * BLK, BLK), F32),
-            pltpu.VMEM((10 * BLK, BLK), F32),
+            pltpu.VMEM((14 * BLK, BLK), F32),
+            pltpu.VMEM((14 * BLK, BLK), F32),
             pltpu.VMEM((SEQ, HD), F32),
             pltpu.VMEM((SEQ, HD), F32),
             pltpu.VMEM((DEVS, 2, 2, HALF, HD), BF),
@@ -376,6 +394,7 @@
             dma((8,)),
             dma,
             dma((2,)),
+            dma((4,)),
         ],
         compiler_params=pltpu.CompilerParams(
             collective_id=0, has_side_effects=True, vmem_limit_bytes=60 * 1024 * 1024

time: 58.3 us -> 57 us (0.978)
  Pallas kernels: 57.6 us -> 56.2 us
    pallas_call x1, Pallas kernels: 56.5 us -> 55.1 us  [on_device(): pl.pallas_call(kernel, name='exchange_attend', out_shape=(pltpu.VMEM((TOK...]
where the time goes in v4:
time: 57 us; the launch traced here: 56.9 us
  Pallas kernels  56.2 us (99%)
  between operations  0.64 us (1%)
    pallas_call x1, Pallas kernels, on_device(): pl.pallas_call(kernel, name='exchange_attend', out_shape=(pltpu.VMEM((TOK...  55.1 us
    pallas_call x1, Pallas kernels, on_device(): pl.pallas_call(put, name='put', out_shape=(jax.ShapeDtypeStruct((TOK, QH...  1.16 us

profile of v4, /device:TPU:1, one launch (start us, length us, event | category | flops | bytes accessed | tf_op | source)
XLA Modules:
  0.0 56.9 jit_solution(18312630054160267464)
XLA Ops:
  0.6 55.1 %exchange_attend.1 = (bf16[128,4096]{1,0:T(8,128)(2,1)S(1)}, bf16[128,1024]{1,0:T(8,128)(2,1)S(1)}, bf16[128,1024]{1,0:T(8,128)(2,1)S(1)}) custom-call(s32[8]{0:T(128)} %lens.1, bf16[128,4096]{1,0:T(8,128)(2,1)} %q_in.1, bf16[128,1024]{1,0:T(8,128)(2,1)} %k_in.1, bf16[128,1024]{1,0:T(8,128)(2,1)} %v_in.1, bf16[128,4096]{1,0:T(8,128)(2,1)} %do_in.1), custom_call_target="tpu_custom_call" | custom-call | tf_op jit(solution)/shard_map/exchange_attend/pallas_call | solution.py:360
  55.7 1.2 %put.1 = (bf16[128,4096]{1,0:T(8,128)(2,1)}, bf16[128,1024]{1,0:T(8,128)(2,1)}, bf16[128,1024]{1,0:T(8,128)(2,1)}) custom-call(bf16[128,4096]{1,0:T(8,128)(2,1)S(1)} %get-tuple-element.6.dq, bf16[128,1024]{1,0:T(8,128)(2,1)S(1)} %get-tuple-element.7.dk, bf16[128,1024]{1,0:T(8,128)(2,1)S(1)} %get-tuple-element.8.dv), custom_call_target="tpu_custom_call" | custom-call | tf_op jit(solution)/shard_map/put/pallas_call | solution.py:403

commit v5 on v4

--- a/solution.py
+++ b/solution.py
@@ -272,8 +272,8 @@
             for w in (b, a):
                 for t in range(w["tiles"]):
                     phase(w, t)
-                if phase is grad_tile:
-                    give_back(h, half, w)
+        for w in (b, a):
+            give_back(h, half, w)
 
     acc = (dka, dva)
     outs = (dk_out, dv_out)

time: 57 us -> 56.8 us (level)
  no operation moved by 1% of the time
where the time goes in v5:
time: 56.8 us; the launch traced here: 56.7 us
  Pallas kernels  56 us (99%)
  between operations  0.64 us (1%)
    pallas_call x1, Pallas kernels, on_device(): pl.pallas_call(kernel, name='exchange_attend', out_shape=(pltpu.VMEM((TOK...  54.9 us
    pallas_call x1, Pallas kernels, on_device(): pl.pallas_call(put, name='put', out_shape=(jax.ShapeDtypeStruct((TOK, QH...  1.16 us

profile of v5, /device:TPU:1, one launch (start us, length us, event | category | flops | bytes accessed | tf_op | source)
XLA Modules:
  0.0 56.7 jit_solution(12473565464469027183)
XLA Ops:
  0.6 54.9 %exchange_attend.1 = (bf16[128,4096]{1,0:T(8,128)(2,1)S(1)}, bf16[128,1024]{1,0:T(8,128)(2,1)S(1)}, bf16[128,1024]{1,0:T(8,128)(2,1)S(1)}) custom-call(s32[8]{0:T(128)} %lens.1, bf16[128,4096]{1,0:T(8,128)(2,1)} %q_in.1, bf16[128,1024]{1,0:T(8,128)(2,1)} %k_in.1, bf16[128,1024]{1,0:T(8,128)(2,1)} %v_in.1, bf16[128,4096]{1,0:T(8,128)(2,1)} %do_in.1), custom_call_target="tpu_custom_call" | custom-call | tf_op jit(solution)/shard_map/exchange_attend/pallas_call | solution.py:360
  55.5 1.2 %put.1 = (bf16[128,4096]{1,0:T(8,128)(2,1)}, bf16[128,1024]{1,0:T(8,128)(2,1)}, bf16[128,1024]{1,0:T(8,128)(2,1)}) custom-call(bf16[128,4096]{1,0:T(8,128)(2,1)S(1)} %get-tuple-element.6.dq, bf16[128,1024]{1,0:T(8,128)(2,1)S(1)} %get-tuple-element.7.dk, bf16[128,1024]{1,0:T(8,128)(2,1)S(1)} %get-tuple-element.8.dv), custom_call_target="tpu_custom_call" | custom-call | tf_op jit(solution)/shard_map/put/pallas_call | solution.py:403
